TPU v7x, 256 devices: a whole 4x4x8 slice. The times are simulated.
256 devices in a mesh: py: 8 (over y, core), pz: 32 (over x, z).
Axes of the slice: x: 4, y: 4, z: 8, core: 2. Of those that a mesh axis runs over, the one named last changes fastest.
Arguments:
- wavefunctions: float32 [2, 8, 128, 128, 128], P(None, None, 'pz', 'py'), may hold values from -6 to 6
- potential: float32 [128, 128, 128], P('pz', 'py'), may hold values from -4 to 4
- cutoff_sq: int32 [1], replicated, may hold values from 2304 to 4096
- locked_mask: int32 [8], replicated, may hold values 0 or 1
Outputs:
- applied: float32 [2, 8, 128, 128, 128], P(None, None, 'pz', 'py')
- rayleigh: float32 [8], replicated
- residual_norm: float32 [8], replicated
All inputs are finite; a program needn't handle non-finite values.
Results may differ from a plain program's by a relative error of at most 0.00005.
Values sent between devices are 32-bit elements; how exact they have to be, the bound alone decides.
A program may use at most 64 MiB of HBM per device.

v0:
```python
import functools
import math

import jax
import jax.numpy as jnp
from jax import lax
from jax.sharding import Mesh
from jax.sharding import PartitionSpec as P

PY = ("py_0", "py_1")
PZ = ("pz_0", "pz_1")
PY_PZ = ("py_0", "py_1", "pz_0", "pz_1")


def split_up(array, dim, peers):
    before, after = (array.shape[:dim], array.shape[dim + 1 :])
    return jnp.moveaxis(array.reshape(*before, peers, -1, *after), dim, 0)


def joined_along(pieces, dim):
    pieces = jnp.moveaxis(pieces, 0, dim)
    dims = pieces.shape
    return pieces.reshape(*dims[:dim], dims[dim] * dims[dim + 1], *dims[dim + 2 :])


def joined_exchange(array, axis, axes, splits, concats):
    sizes = [lax.axis_size(a) for a in axes]
    pieces = split_up(array, splits[0], sizes[0])
    pieces = jnp.moveaxis(split_up(pieces, splits[1] + 1, sizes[1]), 0, 1)
    inside = pieces.shape[2:]
    pieces = pieces.reshape(-1, *inside)
    pieces = lax.all_to_all(pieces, axis, split_axis=0, concat_axis=0, tiled=True)
    pieces = joined_along(pieces.reshape(*sizes, *inside), concats[0] + 1)
    return joined_along(pieces, concats[1])


def one_axis_at_a_time(array, axes):
    return functools.reduce(lax.psum, axes, array)


def make_tables(length, inverse):
    counter = jnp.arange(length, dtype=jnp.int32)
    phase = counter[:, None] * counter[None, :] % length
    angle = 2.0 * math.pi / length * phase.astype(jnp.float32)
    if inverse:
        return (jnp.cos(angle) / length, jnp.sin(angle) / length)
    return (jnp.cos(angle), -jnp.sin(angle))


def transform_axis(field, axis, tables):
    cosines, sines = tables
    letters = "abcdefgh"[: field.ndim - 1]
    place = axis - 1
    source = letters[:place] + "n" + letters[place + 1 :]
    target = letters[:place] + "k" + letters[place + 1 :]
    form = source + ",kn->" + target
    real_part = field[0]
    imag_part = field[1]
    high = lax.Precision.HIGHEST
    out_real = jnp.einsum(form, real_part, cosines, precision=high) - jnp.einsum(
        form, imag_part, sines, precision=high
    )
    out_imag = jnp.einsum(form, real_part, sines, precision=high) + jnp.einsum(
        form, imag_part, cosines, precision=high
    )
    return jnp.stack([out_real, out_imag])


def signed_square(counter, length):
    signed = jnp.where(counter < length // 2, counter, counter - length)
    return signed * signed


def kinetic_table(first_sq, second_sq, third_sq, cutoff_sq, length):
    total = first_sq[:, None, None] + second_sq[None, :, None] + third_sq[None, None, :]
    keep = (total <= cutoff_sq[0]).astype(jnp.float32)
    return 0.5 * (math.pi / length) ** 2 * total.astype(jnp.float32) * keep


def slab_kinetic(field, cutoff_sq, forward, inverse):
    parts, bands, rows_z, rows_y, length = field.shape
    size_y = lax.axis_size(PY)
    size_z = lax.axis_size(PZ)
    along_x = transform_axis(field, 4, forward)
    flat = jnp.moveaxis(along_x, 1, 3).reshape(parts, rows_z, rows_y, bands * length)
    planes = joined_exchange(flat, PY_PZ, (PY, PZ), (3, 3), (2, 1))
    width = planes.shape[3]
    start = lax.axis_index(PY) * (bands * length // size_y) + lax.axis_index(PZ) * width
    column = start + jnp.arange(width, dtype=jnp.int32)
    full_counter = jnp.arange(length, dtype=jnp.int32)
    full_sq = signed_square(full_counter, length)
    kinetic = kinetic_table(
        full_sq, full_sq, signed_square(column % length, length), cutoff_sq, length
    )
    spectrum = transform_axis(transform_axis(planes, 1, forward), 2, forward) * kinetic
    spatial = transform_axis(transform_axis(spectrum, 2, inverse), 1, inverse)
    returned = joined_exchange(spatial, PY_PZ, (PY, PZ), (2, 1), (3, 3))
    ordered = returned.reshape(parts, rows_z, rows_y, size_z, size_y, width)
    ordered = jnp.swapaxes(ordered, 3, 4).reshape(parts, rows_z, rows_y, bands, length)
    return transform_axis(jnp.moveaxis(ordered, 3, 1), 4, inverse)


def apply_kinetic(field, cutoff_sq, forward, inverse):
    return slab_kinetic(field, cutoff_sq, forward, inverse)


def body(wavefunctions, potential, cutoff_sq, locked_mask):
    length = wavefunctions.shape[4]
    forward = make_tables(length, False)
    inverse = make_tables(length, True)
    kinetic_part = apply_kinetic(wavefunctions, cutoff_sq, forward, inverse)
    applied = kinetic_part + potential[None, None] * wavefunctions
    norm_local = jnp.sum(wavefunctions * wavefunctions, axis=(0, 2, 3, 4))
    correlation_local = jnp.sum(wavefunctions * applied, axis=(0, 2, 3, 4))
    applied_local = jnp.sum(applied * applied, axis=(0, 2, 3, 4))
    norm_sq, correlation, applied_sq = (
        one_axis_at_a_time(norm_local, PY_PZ),
        one_axis_at_a_time(correlation_local, PY_PZ),
        one_axis_at_a_time(applied_local, PY_PZ),
    )
    rayleigh = correlation / norm_sq
    residual_sq = applied_sq - rayleigh * correlation
    residual_norm = jnp.sqrt(residual_sq / norm_sq) * (1.0 - locked_mask.astype(jnp.float32))
    return (applied, rayleigh, residual_norm)


def solution(mesh):
    split = Mesh(mesh.devices.reshape(4, 2, 4, 8), ("py_0", "py_1", "pz_0", "pz_1"))
    placed = (P(None, None, PZ, PY, None), P(PZ, PY, None), P(), P())
    return jax.shard_map(
        body,
        mesh=split,
        in_specs=placed,
        out_specs=(P(None, None, PZ, PY, None), P(), P()),
        check_vma=False,
    )
```

profile of v0, /device:TPU:8, one launch (start us, length us, event | category | flops | bytes accessed | tf_op | source)
XLA Modules:
  0.0 175.6 jit_solution(2160928604943075041)
XLA Ops:
  0.6 1.6 fusion.12
  2.2 1.6 fusion.14
  3.8 1.6 fusion.6
  5.4 1.6 fusion.7
  7.0 2.6 %copy.44 = f32[8,2,4,16,128]{3,0,4,2,1:T(8,128)} copy(f32[8,2,4,16,128]{4,3,2,0,1:T(8,128)S(1)} %maximum_bitcast_fusion) | data formatting | bytes 1048576 | tf_op jit(solution)/shard_map/transpose;transpose | solution.py:17
  9.6 5.2 %copy.72 = f32[8,32,2,4,16,4]{4,5,3,2,1,0:T(4,128)} copy(f32[8,32,2,4,16,4]{4,0,5,1,3,2:T(8,128)} %bitcast.168) | data formatting | bytes 1048576 | tf_op jit(solution)/shard_map/reshape | solution.py:31
  14.8 5.4 %reshape.135 = f32[256,1,512]{2,1,0:T(1,128)} reshape(f32[256,2,4,4,16]{4,3,2,1,0:T(4,128)} %bitcast.169) | data formatting | bytes 1048576
  20.3 14.6 %all-to-all-start = ((f32[256,1,512]{2,1,0:T(1,128)}), f32[256,1,512]{2,1,0:T(1,128)S(1)}, u32[]{:S(2)}, u32[]{:S(2)}) async-start(f32[256,1,512]{2,1,0:T(1,128)} %reshape.135), calls=%async_computation | async-start | bytes 1048576 | tf_op jit(solution)/shard_map/all_to_all | solution.py:32
  35.8 19.4 %all-to-all-done = f32[256,1,512]{2,1,0:T(1,128)S(1)} async-done(((f32[256,1,512]{2,1,0:T(1,128)}), f32[256,1,512]{2,1,0:T(1,128)S(1)}, u32[]{:S(2)}, u32[]{:S(2)}) %all-to-all-start) | async-done | bytes 524320 | tf_op jit(solution)/shard_map/all_to_all | solution.py:32
  55.7 1.9 %reduce = f32[256,512]{1,0:T(8,128)S(1)} reduce(f32[256,1,512]{2,1,0:T(1,128)S(1)} %all-to-all-done, f32[]{:T(128)} %broadcast.344), dimensions={1}, to_apply=%all_to_all.6.reduce_sub_computation | reduce | bytes 1048580 | tf_op jit(solution)/shard_map/all_to_all | solution.py:32
  57.6 4.2 %reshape.136 = f32[256,2,4,4,16]{4,3,2,1,0:T(4,128)} reshape(f32[256,512]{1,0:T(8,128)S(1)} %reduce) | data formatting | bytes 1048576
  61.9 3.8 %copy.74 = f32[8,32,2,4,16,4]{1,4,0,5,3,2:T(8,128)S(1)} copy(f32[8,32,2,4,16,4]{4,5,3,2,1,0:T(4,128)} %bitcast.167) | data formatting | bytes 1048576 | tf_op jit(solution)/shard_map/transpose | solution.py:21
  65.7 1.2 fusion.227
  66.9 1.5 copy.49
  68.4 0.6 fusion.39
  69.1 0.6 fusion.50
  70.1 0.7 convolution_subtract_fusion.4
  70.7 0.6 fusion.48
  71.4 0.6 fusion.36
  72.0 0.6 convolution_add_fusion.4
  72.7 0.7 fusion.5
  73.3 0.6 fusion.4
  74.1 0.6 fusion.16
  74.7 0.7 fusion.17
  75.4 0.6 fusion.3
  76.0 0.6 fusion.54
  76.7 0.6 fusion.31
  77.3 0.7 fusion.2
  78.0 0.6 convolution_subtract_fusion.1
  78.6 0.6 convolution_add_fusion.1
  79.3 4.3 %copy.57 = f32[8,2,128,16,4]{3,0,4,2,1:T(8,128)} copy(f32[8,2,128,16,4]{2,3,0,4,1:T(8,128)S(1)} %maximum_bitcast_fusion.1) | data formatting | bytes 1048576 | tf_op jit(solution)/shard_map/transpose | solution.py:17
  83.6 5.3 %copy.77 = f32[8,32,2,4,16,4]{4,5,3,2,1,0:T(4,128)} copy(f32[8,32,2,4,16,4]{4,0,5,3,1,2:T(8,128)} %bitcast.170) | data formatting | bytes 1048576 | tf_op jit(solution)/shard_map/reshape | solution.py:31
  88.9 4.8 %reshape.137 = f32[256,1,512]{2,1,0:T(1,128)S(1)} reshape(f32[256,2,4,4,16]{4,3,2,1,0:T(4,128)} %bitcast.171) | data formatting | bytes 1048576
  93.7 26.6 %all_to_all.10 = f32[256,1,512]{2,1,0:T(1,128)S(1)} all-to-all(f32[256,1,512]{2,1,0:T(1,128)S(1)} %reshape.137), channel_id=1, replica_groups=mesh['py_0'=4,'py_1'=2,'pz_0'=4,'pz_1'=8] {'py_0','py_1','pz_0','pz_1'}, dimensions={0} | all-to-all | bytes 1048576 | tf_op jit(solution)/shard_map/all_to_all | solution.py:32
  120.3 1.9 %reduce.1 = f32[256,512]{1,0:T(8,128)S(1)} reduce(f32[256,1,512]{2,1,0:T(1,128)S(1)} %all_to_all.10, f32[]{:T(128)} %broadcast.344), dimensions={1}, to_apply=%all_to_all.7.reduce_sub_computation | reduce | bytes 1048580 | tf_op jit(solution)/shard_map/all_to_all | solution.py:32
  122.2 4.2 %reshape.138 = f32[256,2,4,4,16]{4,3,2,1,0:T(4,128)} reshape(f32[256,512]{1,0:T(8,128)S(1)} %reduce.1) | data formatting | bytes 1048576
  126.4 6.6 %copy.80 = f32[8,32,2,4,16,4]{4,0,5,1,3,2:T(8,128)} copy(f32[8,32,2,4,16,4]{4,5,3,2,1,0:T(4,128)} %bitcast.172) | data formatting | bytes 1048576 | tf_op jit(solution)/shard_map/transpose | solution.py:99
  133.0 2.8 %copy.63 = f32[2,4,16,8,128]{4,2,1,3,0:T(8,128)S(1)} copy(f32[2,4,16,8,128]{2,3,4,1,0:T(8,128)} %bitcast.173) | data formatting | bytes 1048576 | tf_op jit(solution)/shard_map/reshape | solution.py:99
  135.9 0.6 fusion.19
  136.5 0.6 fusion.18
  137.1 0.6 fusion.1
  137.8 0.6 fusion
  138.4 0.9 multiply_reduce_fusion
  139.3 9.1 %all-reduce.2 = (f32[8]{0:T(128)S(1)}, f32[8]{0:T(128)S(1)}, f32[8]{0:T(128)S(1)}) all-reduce(f32[8]{0:T(128)S(1)} %get-tuple-element.4, f32[8]{0:T(128)S(1)} %get-tuple-element.5, f32[8]{0:T(128)S(1)} %get-tuple-element.3), channel_id=1, replica_groups=mesh['py_0'=4,'py_1'=2,'pz_0'=4,'pz_1'=8] {'py_0'}, use_global_device_ids=true, to_apply=%region_1.2 | all-reduce | flops 24 | bytes 192 | tf_op jit(solution)/shard_map/psum | solution.py:38
  148.4 2.5 %all-reduce.3 = (f32[8]{0:T(128)S(1)}, f32[8]{0:T(128)S(1)}, f32[8]{0:T(128)S(1)}) all-reduce(f32[8]{0:T(128)S(1)} %get-tuple-element.12, f32[8]{0:T(128)S(1)} %get-tuple-element.13, f32[8]{0:T(128)S(1)} %get-tuple-element.14), channel_id=1, replica_groups=mesh['py_0'=4,'py_1'=2,'pz_0'=4,'pz_1'=8] {'py_1'}, use_global_device_ids=true, to_apply=%region_2.3 | all-reduce | flops 24 | bytes 192 | tf_op jit(solution)/shard_map/psum | solution.py:38
  150.9 9.0 %all-reduce.1 = (f32[8]{0:T(128)S(1)}, f32[8]{0:T(128)S(1)}, f32[8]{0:T(128)S(1)}) all-reduce(f32[8]{0:T(128)S(1)} %get-tuple-element.15, f32[8]{0:T(128)S(1)} %get-tuple-element.16, f32[8]{0:T(128)S(1)} %get-tuple-element.17), channel_id=1, replica_groups=mesh['py_0'=4,'py_1'=2,'pz_0'=4,'pz_1'=8] {'pz_0'}, use_global_device_ids=true, to_apply=%region_3.4 | all-reduce | flops 24 | bytes 192 | tf_op jit(solution)/shard_map/psum | solution.py:38
  159.9 15.1 %all-reduce = (f32[8]{0:T(128)S(1)}, f32[8]{0:T(128)S(1)}, f32[8]{0:T(128)S(1)}) all-reduce(f32[8]{0:T(128)S(1)} %get-tuple-element.9, f32[8]{0:T(128)S(1)} %get-tuple-element.10, f32[8]{0:T(128)S(1)} %get-tuple-element.11), channel_id=1, replica_groups=mesh['py_0'=4,'py_1'=2,'pz_0'=4,'pz_1'=8] {'pz_1'}, use_global_device_ids=true, to_apply=%region_4.5 | all-reduce | flops 24 | bytes 192 | tf_op jit(solution)/shard_map/psum | solution.py:38
  175.1 0.5 subtract_multiply_fusion
  (15 shorter events, 1.2 us)
Async XLA Ops:
  20.3 34.9 %all-to-all-start = ((f32[256,1,512]{2,1,0:T(1,128)}), f32[256,1,512]{2,1,0:T(1,128)S(1)}, u32[]{:S(2)}, u32[]{:S(2)}) async-start(f32[256,1,512]{2,1,0:T(1,128)} %reshape.135), calls=%async_computation | async-start | bytes 1048576 | tf_op jit(solution)/shard_map/all_to_all | solution.py:32
  133.0 5.4 %copy-start = (f32[2,8,4,16,128]{4,3,2,1,0:T(8,128)S(1)}, f32[2,8,4,16,128]{4,3,2,1,0:T(8,128)}, u32[]{:S(2)}) copy-start(f32[2,8,4,16,128]{4,3,2,1,0:T(8,128)} %param.4) | copy-start | bytes 1572868
  133.0 5.4 %copy-start.1 = (f32[4,16,128]{2,1,0:T(8,128)S(1)}, f32[4,16,128]{2,1,0:T(8,128)}, u32[]{:S(2)}) copy-start(f32[4,16,128]{2,1,0:T(8,128)} %param.5) | copy-start | bytes 98308
  133.0 42.0 %copy-start.2 = (s32[8]{0:T(128)S(1)}, s32[8]{0:T(128)}, u32[]{:S(2)}) copy-start(s32[8]{0:T(128)} %param.7) | copy-start | bytes 100
where the time goes:
time: 176 us
  blocking collectives  62.3 us (35%)
  local copies, waits for them, and re-layouts  53 us (30%)
  waiting for transfers between devices  19.4 us (11%)
  matrix products  19.1 us (11%)
  starting transfers between devices  14.6 us (8%)
  other arithmetic  5.58 us (3%)
    psum x4, blocking collectives, one_axis_at_a_time(): return functools.reduce(lax.psum, axes, array)  35.7 us
    all_to_all x1, blocking collectives, joined_exchange(): lax.all_to_all(pieces, axis, split_axis=0, concat_axis=0, tiled=True)  26.6 us
    all_to_all x1, waiting for transfers between devices, joined_exchange(): lax.all_to_all(pieces, axis, split_axis=0, concat_axis=0, tiled=True)  19.4 us
    unnamed x10, local copies, waits for them, and re-layouts  18.8 us
    all_to_all x1, starting transfers between devices, joined_exchange(): lax.all_to_all(pieces, axis, split_axis=0, concat_axis=0, tiled=True)  14.6 us
    reshape x2, local copies, waits for them, and re-layouts, joined_exchange(): pieces = pieces.reshape(-1, *inside)  10.5 us
    transpose x1, local copies, waits for them, and re-layouts, slab_kinetic(): jnp.swapaxes(ordered, 3, 4).reshape(parts, rows_z, rows_y, bands, length)  6.59 us
    dot_general x6, matrix products, transform_axis(): jnp.einsum(form, imag_part, sines, precision=high)  4.78 us
  transfers between devices with their start and end apart: 1, of which 1 were waited for; matrix products, arithmetic and copies ran while one was open for 0% of the time, Pallas kernels for 0%

commit v1 on v0

v1 whole, which is shorter than its diff:
```python
import functools
import math

import jax
import jax.numpy as jnp
import numpy as np
from jax import lax
from jax.experimental import pallas as pl
from jax.experimental.pallas import tpu as pltpu
from jax.sharding import PartitionSpec as P

N = 128
NB = 8
NY = 8
NZ = 32
ZL = N // NZ
YL = N // NY
BLK = ZL * (N // NZ)
MESH = pl.DeviceIdType.MESH
F32 = jnp.float32
BF16 = jnp.bfloat16


def basis():
    n = np.arange(N)
    rows = []
    for m in range(N):
        k = (m + 1) // 2
        angle = 2.0 * np.pi * ((k * n) % N) / N
        row = np.cos(angle) if (m % 2 == 1 or m == 0) else np.sin(angle)
        scale = 1.0 / N if k in (0, N // 2) else 2.0 / N
        rows.append(np.sqrt(scale) * row)
    return np.stack(rows)


def high_low(table):
    high = table.astype(BF16)
    low = (table - high.astype(np.float64)).astype(BF16)
    return high, low


def tables():
    f = basis()
    fh, fl = high_low(f)
    right_fwd = np.block([[fh.T, fl.T], [fh.T, fl.T]])
    right_inv = np.block([[fh, fl], [fh, fl]])
    left_fwd = np.block([[fh, fh], [fl, fl]])
    left_inv = np.block([[fh.T, fh.T], [fl.T, fl.T]])
    d = np.zeros((2, N, NZ, 2, ZL))
    for i in range(2):
        d[i, :, :, i, :] = f.reshape(N, NZ, ZL)
    d = d.reshape(2 * N, 2 * N)
    z_fwd = np.concatenate(high_low(d), axis=0)
    z_inv = np.concatenate(high_low(d.T), axis=0)
    return [right_fwd, right_inv, left_fwd, left_inv, z_fwd, z_inv]


def split(x):
    high = x.astype(BF16)
    low = (x - high.astype(F32)).astype(BF16)
    return high, low


def dot(a, b):
    return jnp.dot(a, b, preferred_element_type=F32)


def times_right(x, table):
    high, low = split(x)
    both = dot(jnp.concatenate([high, low], axis=1), table)
    return both[:, :N] + both[:, N:]


def times_left(table, x):
    high, low = split(x)
    both = dot(table, jnp.concatenate([high, low], axis=0))
    return both[:N] + both[N:]


def times_z(table, x):
    high, low = split(x)
    both = dot(table, high)
    return both[: 2 * N] + both[2 * N :] + dot(table[: 2 * N], low)


def kernel(
    u_hbm, v_hbm, cutoff, locked, rf_hbm, ri_hbm, lf_hbm, li_hbm, zf_hbm, zi_hbm,
    out, ray_ref, res_ref,
    u_in, v_in, rf, ri, lf, li, zf, zi,
    planes, pot, sent, got, back, ret, app, kin, row1, row2, tot1, tot2,
    in_sem, y_send, y_recv, z_send, z_recv, b_send, b_recv, o_send, o_recv, o_own, r_send, r_recv,
):
    my = lax.axis_index("py")
    mz = lax.axis_index("pz")

    def y_peer(k):
        return lax.rem(my + k, NY)

    def z_peer(k):
        x = lax.rem(mz // 8 + k // 8, 4)
        z = lax.rem(mz + k, 8)
        return x * 8 + z

    loads = [(u_hbm, u_in), (v_hbm, v_in), (rf_hbm, rf), (lf_hbm, lf), (zf_hbm, zf), (zi_hbm, zi), (li_hbm, li), (ri_hbm, ri)]
    loads = [pltpu.make_async_copy(a, b, in_sem.at[i]) for i, (a, b) in enumerate(loads)]
    for copy in loads:
        copy.start()

    barrier = pltpu.get_barrier_semaphore()

    @pl.loop(1, NZ)
    def _(k):
        pl.semaphore_signal(barrier, inc=1, device_id=(my, z_peer(k)), device_id_type=MESH)

    @pl.loop(1, NY)
    def _(k):
        pl.semaphore_signal(barrier, inc=1, device_id=(y_peer(k), mz), device_id_type=MESH)

    for h in range(2):
        r = lax.broadcasted_iota(jnp.int32, (2 * N, N), 0)
        c = lax.broadcasted_iota(jnp.int32, (2 * N, N), 1)
        ky = (mz * (N // NZ) + 2 * h + r // N + 1) // 2
        kz = (r % N + 1) // 2
        kx = (c + 1) // 2
        s = ky * ky + kz * kz + kx * kx
        kin[:, h * N : (h + 1) * N] = jnp.where(
            s <= cutoff[0], 0.5 * (math.pi / N) ** 2 * s.astype(F32), 0.0
        )

    for copy in loads:
        copy.wait()
    pl.semaphore_wait(barrier, NZ - 1 + NY - 1)

    def drain(ref, sem):
        pltpu.make_async_copy(ref, ref, sem).wait()

    mine = pl.ds(pl.multiple_of(my * YL, YL), YL)
    for part in range(2):
        @pl.loop(1, NY)
        def _(k, part=part):
            j = y_peer(k)
            pltpu.make_async_remote_copy(
                u_in.at[part, j], planes.at[part, :, mine, :], y_send.at[part], y_recv.at[part],
                device_id=(j, mz), device_id_type=MESH,
            ).start()
        planes[part, :, mine, :] = u_in[part, my]

    @pl.loop(1, NY)
    def _(k):
        j = y_peer(k)
        pltpu.make_async_remote_copy(
            v_in, pot.at[:, mine, :], y_send.at[2], y_recv.at[2],
            device_id=(j, mz), device_id_type=MESH,
        ).start()
    pot[:, mine, :] = v_in[...]

    others = pl.ds(0, (NY - 1) * YL)
    rows_mine = pl.ds(pl.multiple_of(mz * BLK, BLK), BLK)
    z_others = pl.ds(0, (NZ - 1) * BLK)

    for part in range(2):
        drain(planes.at[part, :, others, :], y_recv.at[part])
        x = times_right(planes[part].reshape(ZL * N, N), rf[...])
        x = jnp.concatenate([x[z * N : (z + 1) * N] for z in range(ZL)], axis=1)
        x = times_left(lf[...], x)
        for z in range(ZL):
            sent[part, pl.ds(z, N, stride=ZL), :] = x[:, z * N : (z + 1) * N]

        @pl.loop(1, NZ)
        def _(k, part=part):
            d = z_peer(k)
            pltpu.make_async_remote_copy(
                sent.at[part, pl.ds(pl.multiple_of(d * BLK, BLK), BLK), :], got.at[part, rows_mine, :],
                z_send.at[part], z_recv.at[part],
                device_id=(my, d), device_id_type=MESH,
            ).start()
        got[part, rows_mine, :] = sent[part, rows_mine, :]

    for part in range(2):
        drain(got.at[part, z_others, :], z_recv.at[part])
        g = got[part].reshape(NZ, 2, 8, N)
        x = jnp.concatenate([g[:, h].reshape(2 * N, N) for h in range(2)], axis=1)
        x = times_z(zf[...], x) * kin[...]
        x = times_z(zi[...], x)
        x = jnp.stack([x[:, h * N : (h + 1) * N].reshape(NZ, 8, N) for h in range(2)], axis=1)
        back[part] = x.reshape(NZ * BLK, N)

        @pl.loop(1, NZ)
        def _(k, part=part):
            d = z_peer(k)
            pltpu.make_async_remote_copy(
                back.at[part, pl.ds(pl.multiple_of(d * BLK, BLK), BLK), :], ret.at[part, rows_mine, :],
                b_send.at[part], b_recv.at[part],
                device_id=(my, d), device_id_type=MESH,
            ).start()
        ret[part, rows_mine, :] = back[part, rows_mine, :]

    drain(pot.at[:, others, :], y_recv.at[2])
    norm = corr = square = None
    for part in range(2):
        drain(ret.at[part, z_others, :], b_recv.at[part])
        x = jnp.concatenate([ret[part, pl.ds(z, N, stride=ZL), :] for z in range(ZL)], axis=1)
        x = times_left(li[...], x)
        x = jnp.concatenate([x[:, z * N : (z + 1) * N] for z in range(ZL)], axis=0)
        x = times_right(x, ri[...])
        field = planes[part].reshape(ZL * N, N)
        x = x + pot[...].reshape(ZL * N, N) * field
        app[part] = x.reshape(ZL, N, N)

        @pl.loop(1, NY)
        def _(k, part=part):
            j = y_peer(k)
            pltpu.make_async_remote_copy(
                app.at[part, :, pl.ds(pl.multiple_of(j * YL, YL), YL), :], out.at[part, my],
                o_send.at[part], o_recv.at[part],
                device_id=(j, mz), device_id_type=MESH,
            ).start()
        pltpu.make_async_copy(app.at[part, :, mine, :], out.at[part, my], o_own.at[part]).start()
        sums = [jnp.sum(a.reshape(-1, 8, N), axis=0) for a in (field * field, field * x, x * x)]
        if part == 0:
            norm, corr, square = sums
        else:
            norm, corr, square = norm + sums[0], corr + sums[1], square + sums[2]

    lane = lax.broadcasted_iota(jnp.int32, (1, N), 1)
    row = jnp.zeros((1, N), F32)
    for i, value in enumerate((norm, corr, square)):
        row = jnp.where(lane == 16 * i + my, jnp.sum(value), row)
    row1[...] = row
    tot1[mz] = row

    @pl.loop(1, NZ)
    def _(k):
        d = z_peer(k)
        pltpu.make_async_remote_copy(
            row1, tot1.at[mz], r_send.at[0], r_recv.at[0], device_id=(my, d), device_id_type=MESH
        ).start()

    drain(tot1.at[pl.ds(0, NZ - 1)], r_recv.at[0])
    row = jnp.sum(tot1[...], axis=0)
    row2[...] = row
    tot2[my] = row

    @pl.loop(1, NY)
    def _(k):
        j = y_peer(k)
        pltpu.make_async_remote_copy(
            row2, tot2.at[my], r_send.at[1], r_recv.at[1], device_id=(j, mz), device_id_type=MESH
        ).start()

    drain(tot2.at[pl.ds(0, NY - 1)], r_recv.at[1])
    row = jnp.sum(tot2[...], axis=0)
    norm = row[:, 0:NB]
    corr = row[:, 16 : 16 + NB]
    square = row[:, 32 : 32 + NB]
    keep = jnp.zeros((1, NB), F32)
    for b in range(NB):
        keep = jnp.where(lane[:, :NB] == b, 1.0 - locked[b].astype(F32), keep)
    rayleigh = corr / norm
    ray_ref[...] = rayleigh
    res_ref[...] = jnp.sqrt((square - rayleigh * corr) / norm) * keep

    for part in range(2):
        drain(u_in.at[part, pl.ds(0, NY - 1)], y_send.at[part])
        drain(sent.at[part, z_others, :], z_send.at[part])
        drain(back.at[part, z_others, :], b_send.at[part])
        drain(app.at[part, :, others, :], o_send.at[part])
        drain(out.at[part, pl.ds(0, NY - 1)], o_recv.at[part])
        pltpu.make_async_copy(app.at[part, :, mine, :], out.at[part, my], o_own.at[part]).wait()
    drain(pot.at[:, others, :], y_send.at[2])
    drain(tot1.at[pl.ds(0, NZ - 1)], r_send.at[0])
    drain(tot2.at[pl.ds(0, NY - 1)], r_send.at[1])


def body(wavefunctions, potential, cutoff_sq, locked_mask):
    consts = [jnp.asarray(t) for t in tables()]
    any_space = pl.BlockSpec(memory_space=pl.ANY)
    smem = pl.BlockSpec(memory_space=pltpu.SMEM)
    vmem = pl.BlockSpec(memory_space=pltpu.VMEM)
    dma = pltpu.SemaphoreType.DMA
    applied, rayleigh, residual = pl.pallas_call(
        kernel,
        out_shape=(
            jax.ShapeDtypeStruct((2, NB, ZL, YL, N), F32),
            jax.ShapeDtypeStruct((1, NB), F32),
            jax.ShapeDtypeStruct((1, NB), F32),
        ),
        in_specs=[any_space, any_space, smem, smem] + [any_space] * 6,
        out_specs=(any_space, vmem, vmem),
        scratch_shapes=[
            pltpu.VMEM((2, NB, ZL, YL, N), F32),
            pltpu.VMEM((ZL, YL, N), F32),
            *[pltpu.VMEM(t.shape, BF16) for t in consts[:4]],
            pltpu.VMEM((4 * N, 2 * N), BF16),
            pltpu.VMEM((4 * N, 2 * N), BF16),
            pltpu.VMEM((2, ZL, N, N), F32),
            pltpu.VMEM((ZL, N, N), F32),
            pltpu.VMEM((2, NZ * BLK, N), F32),
            pltpu.VMEM((2, NZ * BLK, N), F32),
            pltpu.VMEM((2, NZ * BLK, N), F32),
            pltpu.VMEM((2, NZ * BLK, N), F32),
            pltpu.VMEM((2, ZL, N, N), F32),
            pltpu.VMEM((2 * N, 2 * N), F32),
            pltpu.VMEM((1, N), F32),
            pltpu.VMEM((1, N), F32),
            pltpu.VMEM((NZ, 1, N), F32),
            pltpu.VMEM((NY, 1, N), F32),
            dma((8,)),
            dma((3,)), dma((3,)), dma((2,)), dma((2,)), dma((2,)), dma((2,)),
            dma((2,)), dma((2,)), dma((2,)), dma((2,)), dma((2,)),
        ],
        compiler_params=pltpu.CompilerParams(collective_id=0, has_side_effects=True),
    )(wavefunctions, potential, cutoff_sq, locked_mask, *consts)
    return applied, rayleigh.reshape(NB), residual.reshape(NB)


def solution(mesh):
    placed = (P(None, None, "pz", "py", None), P("pz", "py", None), P(), P())
    return jax.shard_map(
        body,
        mesh=mesh,
        in_specs=placed,
        out_specs=(P(None, None, "pz", "py", None), P(), P()),
        check_vma=False,
    )
```

time: 176 us -> 61.9 us (0.35)
  the two profiles are of different devices: /device:TPU:8 before, /device:TPU:1 now
where the time goes in v1:
time: 61.9 us; the launch traced here: 61.7 us
  Pallas kernels  57.4 us (93%)
  local copies, waits for them, and re-layouts  2.99 us (5%)
  between operations  1.3 us (2%)
    pallas_call x1, Pallas kernels, body(): pl.pallas_call(kernel, out_shape=(jax.ShapeDtypeStruct((2, NB, ZL, YL, N)...  57.4 us
    unnamed x7, local copies, waits for them, and re-layouts  2.99 us

profile of v1, /device:TPU:1, one launch (start us, length us, event | category | flops | bytes accessed | tf_op | source)
XLA Modules:
  0.0 61.7 jit_solution(11890509860573394644)
XLA Ops:
  1.3 57.4 %shard_map.121 = (f32[2,8,4,16,128]{4,3,2,1,0:T(8,128)}, f32[1,8]{1,0:T(1,128)}, f32[1,8]{1,0:T(1,128)}) custom-call(f32[2,8,4,16,128]{4,3,2,1,0:T(8,128)} %u_hbm.1, f32[4,16,128]{2,1,0:T(8,128)} %v_hbm.1, s32[1]{0:T(128)S(6)} %copy.16.cutoff, s32[8]{0:T(128)} %locked.1, bf16[256,256]{1,0:T(8,128)(2,1)} %constant.12.clone.rf_hbm, ...), custom_call_target="tpu_custom_call" | custom-call | tf_op jit(solution)/shard_map/pallas_call | solution.py:281
  58.7 0.0 copy-start.1
  58.7 1.9 %copy.17 = f32[2,8,4,16,128]{4,3,2,1,0:T(8,128)} copy(f32[2,8,4,16,128]{4,3,2,1,0:T(8,128)} %get-tuple-element.12) | data formatting | bytes 1048576
  60.6 0.0 copy-done.1
  60.6 0.0 copy-start
  60.6 0.5 copy.18
  61.1 0.1 copy-done
  61.2 0.5 copy.19
Async XLA Ops:
  58.7 1.9 %copy-start.1 = (f32[1,8]{1,0:T(1,128)S(1)}, f32[1,8]{1,0:T(1,128)}, u32[]{:S(2)}) copy-start(f32[1,8]{1,0:T(1,128)} %get-tuple-element.7) | copy-start | bytes 100
  60.6 0.6 copy-start

commit v2 on v1

v2 whole, which is shorter than its diff:
```python
import functools
import math

import jax
import jax.numpy as jnp
import numpy as np
from jax import lax
from jax.experimental import pallas as pl
from jax.experimental.pallas import tpu as pltpu
from jax.sharding import PartitionSpec as P

N = 128
NB = 8
NY = 8
NZ = 32
ZL = N // NZ
YL = N // NY
BLK = ZL * (N // NZ)
LIVE = 112
FOLD = N - LIVE
HOST = 48
SPHERE = N * N // 4
MESH = pl.DeviceIdType.MESH
F32 = jnp.float32
BF16 = jnp.bfloat16


def basis():
    n = np.arange(N)
    rows = []
    for m in range(N):
        k = (m + 1) // 2
        angle = 2.0 * np.pi * ((k * n) % N) / N
        row = np.cos(angle) if (m % 2 == 1 or m == 0) else np.sin(angle)
        scale = 1.0 / N if k in (0, N // 2) else 2.0 / N
        rows.append(np.sqrt(scale) * row)
    return np.stack(rows)


def high_low(table):
    high = table.astype(BF16)
    low = (table - high.astype(np.float64)).astype(BF16)
    return high, low


def row_order():
    hosts = [2 * k - 1 + c for k in range(HOST, HOST + FOLD // 2) for c in range(2)]
    guests = [2 * (111 - k) - 1 + c for k in range(HOST, HOST + FOLD // 2) for c in range(2)]
    plain = [m for m in range(N) if m not in hosts and m not in guests]
    for host, guest in zip(hosts, guests, strict=True):
        width = [sum(((m + 1) // 2) ** 2 + ((r + 1) // 2) ** 2 <= SPHERE for m in range(N)) for r in (host, guest)]
        assert sum(width) <= N
    return hosts + plain + guests


def tables():
    f = basis()
    fh, fl = high_low(f)
    ph, pl_ = fh[row_order()], fl[row_order()]
    right_fwd = np.block([[fh.T, fl.T], [fh.T, fl.T]])
    right_inv = np.block([[fh, fl], [fh, fl]])
    guest_fwd = np.block([[fh[::-1].T, fl[::-1].T], [fh[::-1].T, fl[::-1].T]])
    guest_inv = np.block([[fh[::-1], fl[::-1]], [fh[::-1], fl[::-1]]])
    left_fwd = np.block([[ph, ph], [pl_, pl_]])
    left_inv = np.block([[ph.T, ph.T], [pl_.T, pl_.T]])
    d = np.zeros((2, N, NZ, 2, ZL))
    for i in range(2):
        d[i, :, :, i, :] = f.reshape(N, NZ, ZL)
    d = d.reshape(2 * N, 2 * N)
    z_fwd = np.concatenate(high_low(d), axis=0)
    z_inv = np.concatenate(high_low(d.T), axis=0)
    return [right_fwd, guest_fwd, left_fwd, right_inv, guest_inv, left_inv, z_fwd, z_inv]


def split(x):
    high = x.astype(BF16)
    low = (x - high.astype(F32)).astype(BF16)
    return high, low


def dot(a, b):
    return jnp.dot(a, b, preferred_element_type=F32)


def times_right(x, table):
    high, low = split(x)
    both = dot(jnp.concatenate([high, low], axis=1), table)
    return both[:, :N] + both[:, N:]


def times_left(table, x):
    high, low = split(x)
    both = dot(table, jnp.concatenate([high, low], axis=0))
    return both[:N] + both[N:]


def times_z(table, x):
    high, low = split(x)
    both = dot(table, high)
    return both[: 2 * N] + both[2 * N :] + dot(table[: 2 * N], low)


def kernel(
    u_hbm, v_hbm, cutoff_hbm, locked_hbm, rf_hbm, gf_hbm, lf_hbm, ri_hbm, gi_hbm, li_hbm, zf_hbm, zi_hbm,
    out, ray_ref, res_ref,
    u_in, v_in, cutoff, locked, rf, gf, lf, ri, gi, li, zf, zi,
    planes, pot, sent, got, back, ret, wave, app, kin, row1, row2, tot1, tot2,
    in_sem, y_send, y_recv, z_send, z_recv, b_send, b_recv, o_send, o_recv, own, r_send, r_recv,
):
    my = lax.axis_index("py")
    mz = lax.axis_index("pz")

    y_chip = [lax.rem(my // 2 + d, 4) * 2 for d in range(4)]
    y_core = [lax.rem(my + d, 2) for d in range(2)]
    y_peers = [y_chip[d] + y_core[c] for d in (2, 1, 3, 0) for c in (0, 1) if d or c]
    z_x = [lax.rem(mz // 8 + d, 4) * 8 for d in range(4)]
    z_z = [lax.rem(mz + d, 8) for d in range(8)]
    z_peers = [(z_x[d] + z_z[e], e % 2) for e in (4, 3, 5, 2, 6, 1, 7, 0) for d in (2, 1, 3, 0) if d or e]

    def load(i, source, target):
        copy = pltpu.make_async_copy(source, target, in_sem.at[i])
        copy.start()
        return copy

    first = [load(0, u_hbm, u_in), load(1, v_hbm, v_in)]
    barrier = pltpu.get_barrier_semaphore()

    for d, _ in z_peers:
        pl.semaphore_signal(barrier, inc=1, device_id=(my, d), device_id_type=MESH)

    for j in y_peers:
        pl.semaphore_signal(barrier, inc=1, device_id=(j, mz), device_id_type=MESH)

    later = [(lf_hbm, lf), (rf_hbm, rf), (gf_hbm, gf), (cutoff_hbm, cutoff), (locked_hbm, locked), (zf_hbm, zf), (zi_hbm, zi), (ri_hbm, ri), (gi_hbm, gi), (li_hbm, li)]
    later = [load(i + 2, a, b) for i, (a, b) in enumerate(later)]
    for copy in first:
        copy.wait()
    with jax.named_scope("barrier"):
        pl.semaphore_wait(barrier, NZ - 1 + NY - 1)

    def drain(ref, sem, name="end"):
        with jax.named_scope(name):
            pltpu.make_async_copy(ref, ref, sem).wait()

    mine = pl.ds(pl.multiple_of(my * YL, YL), YL)
    for part in range(2):
        for j in y_peers:
            pltpu.make_async_remote_copy(
                u_in.at[part, j], planes.at[part, :, mine, :], y_send.at[part], y_recv.at[part],
                device_id=(j, mz), device_id_type=MESH,
            ).start()

    for j in y_peers:
        pltpu.make_async_remote_copy(
            v_in, pot.at[:, mine, :], y_send.at[2], y_recv.at[2],
            device_id=(j, mz), device_id_type=MESH,
        ).start()
    planes[:, :, mine, :] = u_in[:, my]
    pot[:, mine, :] = v_in[...]
    for copy in later:
        copy.wait()

    def first_slot(d, odd, part):
        return 7 * (d // 2) + (4 - part) * odd

    def slots(odd, part):
        return 4 - (odd + part) % 2

    lane = lax.broadcasted_iota(jnp.int32, (1, N), 1)
    up = (lane + 1) // 2
    down = (N - lane) // 2
    for part in range(2):
        start = first_slot(mz, lax.rem(mz, 2), part)
        for h in range(2):
            for i in range(2):
                slot = start + 2 * h + i
                host = slot < FOLD
                ky = jnp.where(host, HOST + slot // 2, jnp.where(slot == LIVE - 1, N // 2, (slot - FOLD + 1) // 2))
                s = ky * ky + up * up
                s = jnp.where(s > jnp.where(host, SPHERE, 4 * SPHERE), (111 - ky) * (111 - ky) + down * down, s)
                kz = (lax.broadcasted_iota(jnp.int32, (N, N), 0) + 1) // 2
                s = s + kz * kz
                kin[part, i * N : (i + 1) * N, h * N : (h + 1) * N] = jnp.where(
                    s <= cutoff[0], 0.5 * (math.pi / N) ** 2 * s.astype(F32), 0.0
                )

    others = pl.ds(0, (NY - 1) * YL)
    own_row = HOST + lax.broadcasted_iota(jnp.int32, (FOLD, N), 0) // 2
    own_kx = (lax.broadcasted_iota(jnp.int32, (FOLD, N), 1) + 1) // 2
    holds = own_row * own_row + own_kx * own_kx <= SPHERE

    def plane_transform(field, target, part):
        x = times_left(lf[...], jnp.concatenate([field[z] for z in range(ZL)], axis=1))
        x = [x[:, z * N : (z + 1) * N] for z in range(ZL)]
        guest = times_right(jnp.concatenate([a[LIVE:] for a in x], axis=0), gf[...])
        live = times_right(jnp.concatenate([a[:LIVE] for a in x], axis=0), rf[...])
        for z in range(ZL):
            a = live[z * LIVE : (z + 1) * LIVE]
            a = jnp.concatenate([jnp.where(holds, a[:FOLD], guest[z * FOLD : (z + 1) * FOLD]), a[FOLD:]], axis=0)
            target[part, pl.ds(z, LIVE, stride=ZL), :] = a

    def by_parity(act):
        for odd in range(2):
            pl.when(lax.rem(mz, 2) == odd)(functools.partial(act, odd))

    def rows(first, count, step):
        return pl.ds(pl.multiple_of(first * step, step), count * ZL)

    def z_out(part, odd):
        def copy_of(d, o):
            count = slots(o, part)
            return sent.at[part, rows(first_slot(d, o, part), count, ZL), :], got.at[part, rows(mz, count, BLK), :]

        for d, e in z_peers:
            a, b = copy_of(d, (odd + e) % 2)
            pltpu.make_async_remote_copy(
                a, b, z_send.at[part], z_recv.at[part], device_id=(my, d), device_id_type=MESH
            ).start()
        pltpu.make_async_copy(*copy_of(mz, odd), own.at[part]).start()

    def z_back(part, odd):
        count = slots(odd, part)
        target = ret.at[part, rows(first_slot(mz, odd, part), count, ZL), :]
        for d, _ in z_peers:
            pltpu.make_async_remote_copy(
                back.at[part, rows(d, count, BLK), :], target, b_send.at[part], b_recv.at[part],
                device_id=(my, d), device_id_type=MESH,
            ).start()
        pltpu.make_async_copy(back.at[part, rows(mz, count, BLK), :], target, own.at[2 + part]).start()

    def z_rows(part, odd):
        return got.at[part, pl.ds(0, (NZ - 1) * ZL * slots(odd, part)), :]

    def slot_rows(part, odd):
        return ret.at[part, pl.ds(0, ZL * (LIVE - slots(odd, part))), :]

    def z_wait(part, odd):
        drain(z_rows(part, odd), z_recv.at[part], f"z{part}")
        pltpu.make_async_copy(back.at[part, rows(0, slots(odd, part), BLK), :], got.at[part, rows(0, slots(odd, part), BLK), :], own.at[part]).wait()

    def b_wait(part, odd):
        drain(slot_rows(part, odd), b_recv.at[part], f"b{part}")
        pltpu.make_async_copy(back.at[part, rows(0, slots(odd, part), BLK), :], got.at[part, rows(0, slots(odd, part), BLK), :], own.at[2 + part]).wait()

    for part in range(2):
        drain(planes.at[part, :, others, :], y_recv.at[part], f"y{part}")
        plane_transform(planes[part], sent, part)
        by_parity(functools.partial(z_out, part))

    def folded(x):
        return jnp.sum(x.reshape(-1, 8, N), axis=0)

    drain(pot.at[:, others, :], y_recv.at[2], "pot")
    norm = corr = square = jnp.zeros((8, N), F32)
    for part in range(2):
        field = planes[part]
        local = pot[...] * field
        norm = norm + folded(field * field)
        corr = corr + folded(field * local)
        square = square + folded(local * local)
        plane_transform(local, wave, part)

    upper = lax.rem(lax.broadcasted_iota(jnp.int32, (2 * N, N), 0), 2 * ZL) < ZL
    for part in range(2):
        by_parity(functools.partial(z_wait, part))
        g = got[part].reshape(NZ, 2, 8, N)
        g = [g[:, h].reshape(2 * N, N) for h in range(2)]
        g[1] = jnp.where(upper | (lax.rem(mz + part, 2) == 0), g[1], 0.0)
        x = times_z(zf[...], jnp.concatenate(g, axis=1)) * kin[part]
        x = times_z(zi[...], x)
        x = jnp.stack([x[:, h * N : (h + 1) * N].reshape(NZ, 8, N) for h in range(2)], axis=1)
        back[part] = x.reshape(NZ * BLK, N)
        by_parity(functools.partial(z_back, part))

    for part in range(2):
        by_parity(functools.partial(b_wait, part))
        x = ret[part]
        corr = corr + folded(sent[part] * x)
        square = square + folded(x * (x + 2.0 * wave[part]))
        if part == 1:
            row = jnp.zeros((1, N), F32)
            for i, value in enumerate((norm, corr, square)):
                total = jnp.sum(jnp.sum(value, axis=0, keepdims=True), axis=1, keepdims=True)
                row = jnp.where(lane == 16 * i + my, total, row)
            row1[...] = row
            tot1[mz] = row

            for d, _ in z_peers:
                pltpu.make_async_remote_copy(
                    row1, tot1.at[mz], r_send.at[0], r_recv.at[0], device_id=(my, d), device_id_type=MESH
                ).start()

        x = [ret[part, pl.ds(z, LIVE, stride=ZL), :] for z in range(ZL)]
        guest = times_right(jnp.concatenate([jnp.where(holds, 0.0, a[:FOLD]) for a in x], axis=0), gi[...])
        live = [b for a in x for b in (jnp.where(holds, a[:FOLD], 0.0), a[FOLD:])]
        live = times_right(jnp.concatenate(live, axis=0), ri[...])
        x = [
            jnp.concatenate([live[z * LIVE : (z + 1) * LIVE], guest[z * FOLD : (z + 1) * FOLD]], axis=0)
            for z in range(ZL)
        ]
        x = times_left(li[...], jnp.concatenate(x, axis=1))
        for z in range(ZL):
            app[part, z] = x[:, z * N : (z + 1) * N] + pot[z] * planes[part, z]

        for j in y_peers:
            pltpu.make_async_remote_copy(
                app.at[part, :, pl.ds(pl.multiple_of(j * YL, YL), YL), :], out.at[part, my],
                o_send.at[part], o_recv.at[part],
                device_id=(j, mz), device_id_type=MESH,
            ).start()
        out[part, my] = app[part, :, mine, :]

    drain(tot1.at[pl.ds(0, NZ - 1)], r_recv.at[0], "r0")
    row = jnp.sum(tot1[...], axis=0)
    row2[...] = row
    tot2[my] = row

    for j in y_peers:
        pltpu.make_async_remote_copy(
            row2, tot2.at[my], r_send.at[1], r_recv.at[1], device_id=(j, mz), device_id_type=MESH
        ).start()

    for part in range(2):
        drain(u_in.at[part, pl.ds(0, NY - 1)], y_send.at[part])
        by_parity(lambda odd, part=part: drain(slot_rows(part, odd), z_send.at[part]))
        by_parity(lambda odd, part=part: drain(z_rows(part, odd), b_send.at[part]))
        drain(app.at[part, :, others, :], o_send.at[part])
        drain(out.at[part, pl.ds(0, NY - 1)], o_recv.at[part], f"o{part}")
    drain(pot.at[:, others, :], y_send.at[2])
    drain(tot1.at[pl.ds(0, NZ - 1)], r_send.at[0])

    keep = jnp.zeros((1, NB), F32)
    for b in range(NB):
        keep = jnp.where(lane[:, :NB] == b, 1.0 - locked[b].astype(F32), keep)
    drain(tot2.at[pl.ds(0, NY - 1)], r_recv.at[1], "r1")
    row = jnp.sum(tot2[...], axis=0)
    norm = row[:, 0:NB]
    corr = row[:, 16 : 16 + NB]
    square = row[:, 32 : 32 + NB]
    rayleigh = corr / norm
    ray_ref[...] = rayleigh.reshape(NB)
    res_ref[...] = (jnp.sqrt((square - rayleigh * corr) / norm) * keep).reshape(NB)
    drain(tot2.at[pl.ds(0, NY - 1)], r_send.at[1])


def write_out(applied, rayleigh, residual, *rest):
    sources, sem = (applied, rayleigh, residual), rest[3]
    copies = [pltpu.make_async_copy(a, b, sem.at[i]) for i, (a, b) in enumerate(zip(sources, rest[:3], strict=True))]
    for copy in copies:
        copy.start()
    for copy in copies:
        copy.wait()


def body(wavefunctions, potential, cutoff_sq, locked_mask):
    consts = [jnp.asarray(t) for t in tables()]
    hbm = pl.BlockSpec(memory_space=pltpu.HBM)
    vmem = pl.BlockSpec(memory_space=pltpu.VMEM)
    dma = pltpu.SemaphoreType.DMA
    applied, rayleigh, residual = pl.pallas_call(
        kernel,
        out_shape=(
            pltpu.VMEM((2, NB, ZL, YL, N), F32),
            pltpu.VMEM((NB,), F32),
            pltpu.VMEM((NB,), F32),
        ),
        in_specs=[hbm] * 12,
        out_specs=(vmem, vmem, vmem),
        scratch_shapes=[
            pltpu.VMEM((2, NB, ZL, YL, N), F32),
            pltpu.VMEM((ZL, YL, N), F32),
            pltpu.SMEM((1,), jnp.int32),
            pltpu.SMEM((NB,), jnp.int32),
            *[pltpu.VMEM(t.shape, BF16) for t in consts],
            pltpu.VMEM((2, ZL, N, N), F32),
            pltpu.VMEM((ZL, N, N), F32),
            pltpu.VMEM((2, LIVE * ZL, N), F32),
            pltpu.VMEM((2, NZ * BLK, N), F32),
            pltpu.VMEM((2, NZ * BLK, N), F32),
            pltpu.VMEM((2, LIVE * ZL, N), F32),
            pltpu.VMEM((2, LIVE * ZL, N), F32),
            pltpu.VMEM((2, ZL, N, N), F32),
            pltpu.VMEM((2, 2 * N, 2 * N), F32),
            pltpu.VMEM((1, N), F32),
            pltpu.VMEM((1, N), F32),
            pltpu.VMEM((NZ, 1, N), F32),
            pltpu.VMEM((NY, 1, N), F32),
            dma((12,)),
            dma((3,)), dma((3,)), dma((2,)), dma((2,)), dma((2,)), dma((2,)),
            dma((2,)), dma((2,)), dma((4,)), dma((2,)), dma((2,)),
        ],
        compiler_params=pltpu.CompilerParams(collective_id=0, has_side_effects=True),
    )(wavefunctions, potential, cutoff_sq, locked_mask, *consts)
    return pl.pallas_call(
        write_out,
        out_shape=(
            jax.ShapeDtypeStruct((2, NB, ZL, YL, N), F32),
            jax.ShapeDtypeStruct((NB,), F32),
            jax.ShapeDtypeStruct((NB,), F32),
        ),
        in_specs=[vmem] * 3,
        out_specs=(hbm,) * 3,
        scratch_shapes=[dma((3,))],
    )(*[pltpu.with_memory_space_constraint(a, pltpu.VMEM) for a in (applied, rayleigh, residual)])


def solution(mesh):
    placed = (P(None, None, "pz", "py", None), P("pz", "py", None), P(), P())
    return jax.shard_map(
        body,
        mesh=mesh,
        in_specs=placed,
        out_specs=(P(None, None, "pz", "py", None), P(), P()),
        check_vma=False,
    )
```

time: 61.9 us -> 53 us (0.86)
  Pallas kernels: 57.4 us -> 51.6 us
  local copies, waits for them, and re-layouts: 2.99 us -> 0 us
    pallas_call x1 -> x2, Pallas kernels: 57.4 us -> 51.6 us  [the longest x1 50.8 us: body(): pl.pallas_call(kernel, out_shape=(pltpu.VMEM((2, NB, ZL, YL, N), F32), pl...]
    unnamed x7 -> x0, local copies, waits for them, and re-layouts: 2.99 us -> none
where the time goes in v2:
time: 53 us; the launch traced here: 52.9 us
  Pallas kernels  51.6 us (97%)
  between operations  1.28 us (2%)
    pallas_call x1, Pallas kernels, body(): pl.pallas_call(kernel, out_shape=(pltpu.VMEM((2, NB, ZL, YL, N), F32), pl...  50.8 us

profile of v2, /device:TPU:1, one launch (start us, length us, event | category | flops | bytes accessed | tf_op | source)
XLA Modules:
  0.0 52.9 jit_solution(8126847929089143215)
XLA Ops:
  1.3 50.8 %shard_map.139 = (f32[2,8,4,16,128]{4,3,2,1,0:T(8,128)S(1)}, f32[8]{0:T(128)S(1)}, f32[8]{0:T(128)S(1)}) custom-call(f32[2,8,4,16,128]{4,3,2,1,0:T(8,128)} %u_hbm.1, f32[4,16,128]{2,1,0:T(8,128)} %v_hbm.1, s32[1]{0:T(128)S(6)} %copy.15.cutoff_hbm, s32[8]{0:T(128)} %locked_hbm.1, bf16[256,256]{1,0:T(8,128)(2,1)} %constant.16.clone.rf_hbm, ...), custom_call_target="tpu_custom_call" | custom-call | tf_op jit(solution)/shard_map/pallas_call | solution.py:360
  52.0 0.8 %shard_map.140 = (f32[2,8,4,16,128]{4,3,2,1,0:T(8,128)}, f32[8]{0:T(128)}, f32[8]{0:T(128)}) custom-call(f32[2,8,4,16,128]{4,3,2,1,0:T(8,128)S(1)} %get-tuple-element.6.applied, f32[8]{0:T(128)S(1)} %get-tuple-element.7.rayleigh, f32[8]{0:T(128)S(1)} %get-tuple-element.8.residual), custom_call_target="tpu_custom_call" | custom-call | tf_op jit(solution)/shard_map/pallas_call | solution.py:394

commit v3 on v2

--- a/solution.py
+++ b/solution.py
@@ -15,7 +15,8 @@
 NZ = 32
 ZL = N // NZ
 YL = N // NY
-BLK = ZL * (N // NZ)
+SL = N // NZ
+CHUNKS = ((0, 0, 1), (0, 1, 1), (0, 2, 2), (1, 0, 4))
 LIVE = 112
 FOLD = N - LIVE
 HOST = 48
@@ -63,12 +64,9 @@
     guest_inv = np.block([[fh[::-1], fl[::-1]], [fh[::-1], fl[::-1]]])
     left_fwd = np.block([[ph, ph], [pl_, pl_]])
     left_inv = np.block([[ph.T, ph.T], [pl_.T, pl_.T]])
-    d = np.zeros((2, N, NZ, 2, ZL))
-    for i in range(2):
-        d[i, :, :, i, :] = f.reshape(N, NZ, ZL)
-    d = d.reshape(2 * N, 2 * N)
-    z_fwd = np.concatenate(high_low(d), axis=0)
-    z_inv = np.concatenate(high_low(d.T), axis=0)
+    zh, zl = (t.reshape(N, NZ, ZL).swapaxes(1, 2).reshape(N, N) for t in (fh, fl))
+    z_fwd = np.block([[zh, zh], [zl, zl]])
+    z_inv = np.block([[zh.T, zh.T], [zl.T, zl.T]])
     return [right_fwd, guest_fwd, left_fwd, right_inv, guest_inv, left_inv, z_fwd, z_inv]
 
 
@@ -92,12 +90,6 @@
     high, low = split(x)
     both = dot(table, jnp.concatenate([high, low], axis=0))
     return both[:N] + both[N:]
-
-
-def times_z(table, x):
-    high, low = split(x)
-    both = dot(table, high)
-    return both[: 2 * N] + both[2 * N :] + dot(table[: 2 * N], low)
 
 
 def kernel(
@@ -143,16 +135,16 @@
             pltpu.make_async_copy(ref, ref, sem).wait()
 
     mine = pl.ds(pl.multiple_of(my * YL, YL), YL)
-    for part in range(2):
+    for c, (part, z, nz) in enumerate(CHUNKS):
         for j in y_peers:
             pltpu.make_async_remote_copy(
-                u_in.at[part, j], planes.at[part, :, mine, :], y_send.at[part], y_recv.at[part],
+                u_in.at[part, j, pl.ds(z, nz)], planes.at[part, pl.ds(z, nz), mine, :], y_send.at[c], y_recv.at[c],
                 device_id=(j, mz), device_id_type=MESH,
             ).start()
 
     for j in y_peers:
         pltpu.make_async_remote_copy(
-            v_in, pot.at[:, mine, :], y_send.at[2], y_recv.at[2],
+            v_in, pot.at[:, mine, :], y_send.at[len(CHUNKS)], y_recv.at[len(CHUNKS)],
             device_id=(j, mz), device_id_type=MESH,
         ).start()
     planes[:, :, mine, :] = u_in[:, my]
@@ -171,86 +163,94 @@
     down = (N - lane) // 2
     for part in range(2):
         start = first_slot(mz, lax.rem(mz, 2), part)
-        for h in range(2):
-            for i in range(2):
-                slot = start + 2 * h + i
-                host = slot < FOLD
-                ky = jnp.where(host, HOST + slot // 2, jnp.where(slot == LIVE - 1, N // 2, (slot - FOLD + 1) // 2))
-                s = ky * ky + up * up
-                s = jnp.where(s > jnp.where(host, SPHERE, 4 * SPHERE), (111 - ky) * (111 - ky) + down * down, s)
-                kz = (lax.broadcasted_iota(jnp.int32, (N, N), 0) + 1) // 2
-                s = s + kz * kz
-                kin[part, i * N : (i + 1) * N, h * N : (h + 1) * N] = jnp.where(
-                    s <= cutoff[0], 0.5 * (math.pi / N) ** 2 * s.astype(F32), 0.0
-                )
+        for i in range(SL):
+            slot = start + i
+            host = slot < FOLD
+            ky = jnp.where(host, HOST + slot // 2, jnp.where(slot == LIVE - 1, N // 2, (slot - FOLD + 1) // 2))
+            s = ky * ky + up * up
+            s = jnp.where(s > jnp.where(host, SPHERE, 4 * SPHERE), (111 - ky) * (111 - ky) + down * down, s)
+            kz = (lax.broadcasted_iota(jnp.int32, (N, N), 0) + 1) // 2
+            s = s + kz * kz
+            kin[part, :, i * N : (i + 1) * N] = jnp.where(
+                s <= cutoff[0], 0.5 * (math.pi / N) ** 2 * s.astype(F32), 0.0
+            )
 
     others = pl.ds(0, (NY - 1) * YL)
     own_row = HOST + lax.broadcasted_iota(jnp.int32, (FOLD, N), 0) // 2
     own_kx = (lax.broadcasted_iota(jnp.int32, (FOLD, N), 1) + 1) // 2
     holds = own_row * own_row + own_kx * own_kx <= SPHERE
 
-    def plane_transform(field, target, part):
-        x = times_left(lf[...], jnp.concatenate([field[z] for z in range(ZL)], axis=1))
-        x = [x[:, z * N : (z + 1) * N] for z in range(ZL)]
+    def plane_transform(field, target, part, first, count):
+        x = times_left(lf[...], jnp.concatenate([field[z] for z in range(count)], axis=1))
+        x = [x[:, z * N : (z + 1) * N] for z in range(count)]
         guest = times_right(jnp.concatenate([a[LIVE:] for a in x], axis=0), gf[...])
         live = times_right(jnp.concatenate([a[:LIVE] for a in x], axis=0), rf[...])
-        for z in range(ZL):
+        for z in range(count):
             a = live[z * LIVE : (z + 1) * LIVE]
-            a = jnp.concatenate([jnp.where(holds, a[:FOLD], guest[z * FOLD : (z + 1) * FOLD]), a[FOLD:]], axis=0)
-            target[part, pl.ds(z, LIVE, stride=ZL), :] = a
+            target[part, first + z, :FOLD, :] = jnp.where(holds, a[:FOLD], guest[z * FOLD : (z + 1) * FOLD])
+            target[part, first + z, FOLD:, :] = a[FOLD:]
 
     def by_parity(act):
         for odd in range(2):
             pl.when(lax.rem(mz, 2) == odd)(functools.partial(act, odd))
 
-    def rows(first, count, step):
-        return pl.ds(pl.multiple_of(first * step, step), count * ZL)
-
-    def z_out(part, odd):
+    got_view = got.reshape(2, NZ, ZL, SL, N)
+    back_view = back.reshape(2, NZ, ZL, SL, N)
+
+    def z_out(part, first, count, c, odd):
         def copy_of(d, o):
-            count = slots(o, part)
-            return sent.at[part, rows(first_slot(d, o, part), count, ZL), :], got.at[part, rows(mz, count, BLK), :]
+            n = slots(o, part)
+            return (
+                sent.at[part, pl.ds(first, count), pl.ds(first_slot(d, o, part), n), :],
+                got_view.at[part, mz, pl.ds(first, count), pl.ds(0, n), :],
+            )
 
         for d, e in z_peers:
             a, b = copy_of(d, (odd + e) % 2)
             pltpu.make_async_remote_copy(
                 a, b, z_send.at[part], z_recv.at[part], device_id=(my, d), device_id_type=MESH
             ).start()
-        pltpu.make_async_copy(*copy_of(mz, odd), own.at[part]).start()
+        pltpu.make_async_copy(*copy_of(mz, odd), own.at[c]).start()
 
     def z_back(part, odd):
-        count = slots(odd, part)
-        target = ret.at[part, rows(first_slot(mz, odd, part), count, ZL), :]
+        n = slots(odd, part)
+        target = ret.at[part, :, pl.ds(first_slot(mz, odd, part), n), :]
         for d, _ in z_peers:
             pltpu.make_async_remote_copy(
-                back.at[part, rows(d, count, BLK), :], target, b_send.at[part], b_recv.at[part],
+                back_view.at[part, d, :, pl.ds(0, n), :], target, b_send.at[part], b_recv.at[part],
                 device_id=(my, d), device_id_type=MESH,
             ).start()
-        pltpu.make_async_copy(back.at[part, rows(mz, count, BLK), :], target, own.at[2 + part]).start()
+        pltpu.make_async_copy(back_view.at[part, mz, :, pl.ds(0, n), :], target, own.at[len(CHUNKS) + part]).start()
 
     def z_rows(part, odd):
-        return got.at[part, pl.ds(0, (NZ - 1) * ZL * slots(odd, part)), :]
+        return got_view.at[part, pl.ds(0, NZ - 1), :, pl.ds(0, slots(odd, part)), :]
 
     def slot_rows(part, odd):
-        return ret.at[part, pl.ds(0, ZL * (LIVE - slots(odd, part))), :]
+        return ret.at[part, :, pl.ds(0, LIVE - slots(odd, part)), :]
+
+    def own_wait(part, count, c, odd):
+        a = ret.at[part, pl.ds(0, count), pl.ds(0, slots(odd, part)), :]
+        pltpu.make_async_copy(a, a, own.at[c]).wait()
 
     def z_wait(part, odd):
         drain(z_rows(part, odd), z_recv.at[part], f"z{part}")
-        pltpu.make_async_copy(back.at[part, rows(0, slots(odd, part), BLK), :], got.at[part, rows(0, slots(odd, part), BLK), :], own.at[part]).wait()
+        for c, (p, _, count) in enumerate(CHUNKS):
+            if p == part:
+                own_wait(part, count, c, odd)
 
     def b_wait(part, odd):
         drain(slot_rows(part, odd), b_recv.at[part], f"b{part}")
-        pltpu.make_async_copy(back.at[part, rows(0, slots(odd, part), BLK), :], got.at[part, rows(0, slots(odd, part), BLK), :], own.at[2 + part]).wait()
-
-    for part in range(2):
-        drain(planes.at[part, :, others, :], y_recv.at[part], f"y{part}")
-        plane_transform(planes[part], sent, part)
-        by_parity(functools.partial(z_out, part))
+        own_wait(part, ZL, len(CHUNKS) + part, odd)
+
+    for c, (part, z, nz) in enumerate(CHUNKS):
+        drain(planes.at[part, pl.ds(z, nz), others, :], y_recv.at[c], f"y{c}")
+        plane_transform(planes[part, z : z + nz], sent, part, z, nz)
+        by_parity(functools.partial(z_out, part, z, nz, c))
 
     def folded(x):
         return jnp.sum(x.reshape(-1, 8, N), axis=0)
 
-    drain(pot.at[:, others, :], y_recv.at[2], "pot")
+    drain(pot.at[:, others, :], y_recv.at[len(CHUNKS)], "pot")
     norm = corr = square = jnp.zeros((8, N), F32)
     for part in range(2):
         field = planes[part]
@@ -258,18 +258,19 @@
         norm = norm + folded(field * field)
         corr = corr + folded(field * local)
         square = square + folded(local * local)
-        plane_transform(local, wave, part)
-
-    upper = lax.rem(lax.broadcasted_iota(jnp.int32, (2 * N, N), 0), 2 * ZL) < ZL
+        plane_transform(local, wave, part, 0, ZL)
+
     for part in range(2):
         by_parity(functools.partial(z_wait, part))
-        g = got[part].reshape(NZ, 2, 8, N)
-        g = [g[:, h].reshape(2 * N, N) for h in range(2)]
-        g[1] = jnp.where(upper | (lax.rem(mz + part, 2) == 0), g[1], 0.0)
-        x = times_z(zf[...], jnp.concatenate(g, axis=1)) * kin[part]
-        x = times_z(zi[...], x)
-        x = jnp.stack([x[:, h * N : (h + 1) * N].reshape(NZ, 8, N) for h in range(2)], axis=1)
-        back[part] = x.reshape(NZ * BLK, N)
+        x = [
+            jnp.concatenate([got[part, pl.ds(SL * z + i, NZ, stride=SL * ZL), :] for z in range(ZL)], axis=0)
+            for i in range(SL)
+        ]
+        x = times_left(zf[...], jnp.concatenate(x, axis=1)) * kin[part]
+        x = times_left(zi[...], x)
+        for z in range(ZL):
+            for i in range(SL):
+                back[part, pl.ds(SL * z + i, NZ, stride=SL * ZL), :] = x[z * NZ : (z + 1) * NZ, i * N : (i + 1) * N]
         by_parity(functools.partial(z_back, part))
 
     for part in range(2):
@@ -290,7 +291,7 @@
                     row1, tot1.at[mz], r_send.at[0], r_recv.at[0], device_id=(my, d), device_id_type=MESH
                 ).start()
 
-        x = [ret[part, pl.ds(z, LIVE, stride=ZL), :] for z in range(ZL)]
+        x = [ret[part, z] for z in range(ZL)]
         guest = times_right(jnp.concatenate([jnp.where(holds, 0.0, a[:FOLD]) for a in x], axis=0), gi[...])
         live = [b for a in x for b in (jnp.where(holds, a[:FOLD], 0.0), a[FOLD:])]
         live = times_right(jnp.concatenate(live, axis=0), ri[...])
@@ -321,12 +322,13 @@
         ).start()
 
     for part in range(2):
-        drain(u_in.at[part, pl.ds(0, NY - 1)], y_send.at[part])
         by_parity(lambda odd, part=part: drain(slot_rows(part, odd), z_send.at[part]))
         by_parity(lambda odd, part=part: drain(z_rows(part, odd), b_send.at[part]))
         drain(app.at[part, :, others, :], o_send.at[part])
         drain(out.at[part, pl.ds(0, NY - 1)], o_recv.at[part], f"o{part}")
-    drain(pot.at[:, others, :], y_send.at[2])
+    drain(pot.at[:, others, :], y_send.at[len(CHUNKS)])
+    for c, (part, z, nz) in enumerate(CHUNKS):
+        drain(planes.at[part, pl.ds(z, nz), others, :], y_send.at[c])
     drain(tot1.at[pl.ds(0, NZ - 1)], r_send.at[0])
 
     keep = jnp.zeros((1, NB), F32)
@@ -374,20 +376,20 @@
             *[pltpu.VMEM(t.shape, BF16) for t in consts],
             pltpu.VMEM((2, ZL, N, N), F32),
             pltpu.VMEM((ZL, N, N), F32),
-            pltpu.VMEM((2, LIVE * ZL, N), F32),
-            pltpu.VMEM((2, NZ * BLK, N), F32),
-            pltpu.VMEM((2, NZ * BLK, N), F32),
-            pltpu.VMEM((2, LIVE * ZL, N), F32),
-            pltpu.VMEM((2, LIVE * ZL, N), F32),
+            pltpu.VMEM((2, ZL, LIVE, N), F32),
+            pltpu.VMEM((2, NZ * ZL * SL, N), F32),
+            pltpu.VMEM((2, NZ * ZL * SL, N), F32),
+            pltpu.VMEM((2, ZL, LIVE, N), F32),
+            pltpu.VMEM((2, ZL, LIVE, N), F32),
             pltpu.VMEM((2, ZL, N, N), F32),
-            pltpu.VMEM((2, 2 * N, 2 * N), F32),
+            pltpu.VMEM((2, N, SL * N), F32),
             pltpu.VMEM((1, N), F32),
             pltpu.VMEM((1, N), F32),
             pltpu.VMEM((NZ, 1, N), F32),
             pltpu.VMEM((NY, 1, N), F32),
             dma((12,)),
-            dma((3,)), dma((3,)), dma((2,)), dma((2,)), dma((2,)), dma((2,)),
-            dma((2,)), dma((2,)), dma((4,)), dma((2,)), dma((2,)),
+            dma((len(CHUNKS) + 1,)), dma((len(CHUNKS) + 1,)), dma((2,)), dma((2,)), dma((2,)), dma((2,)),
+            dma((2,)), dma((2,)), dma((len(CHUNKS) + 2,)), dma((2,)), dma((2,)),
         ],
         compiler_params=pltpu.CompilerParams(collective_id=0, has_side_effects=True),
     )(wavefunctions, potential, cutoff_sq, locked_mask, *consts)

time: 53 us -> 51.4 us (0.970)
  Pallas kernels: 51.6 us -> 50 us
    pallas_call x1, Pallas kernels: 50.8 us -> 49.2 us  [body(): pl.pallas_call(kernel, out_shape=(pltpu.VMEM((2, NB, ZL, YL, N), F32), pl...]
where the time goes in v3:
time: 51.4 us; the launch traced here: 51.3 us
  Pallas kernels  50 us (97%)
  between operations  1.28 us (2%)
    pallas_call x1, Pallas kernels, body(): pl.pallas_call(kernel, out_shape=(pltpu.VMEM((2, NB, ZL, YL, N), F32), pl...  49.2 us

profile of v3, /device:TPU:1, one launch (start us, length us, event | category | flops | bytes accessed | tf_op | source)
XLA Modules:
  0.0 51.3 jit_solution(9152783018655592328)
XLA Ops:
  1.3 49.2 %shard_map.139 = (f32[2,8,4,16,128]{4,3,2,1,0:T(8,128)S(1)}, f32[8]{0:T(128)S(1)}, f32[8]{0:T(128)S(1)}) custom-call(f32[2,8,4,16,128]{4,3,2,1,0:T(8,128)} %u_hbm.1, f32[4,16,128]{2,1,0:T(8,128)} %v_hbm.1, s32[1]{0:T(128)S(6)} %copy.15.cutoff_hbm, s32[8]{0:T(128)} %locked_hbm.1, bf16[256,256]{1,0:T(8,128)(2,1)} %constant.16.clone.rf_hbm, ...), custom_call_target="tpu_custom_call" | custom-call | tf_op jit(solution)/shard_map/pallas_call | solution.py:362
  50.5 0.8 %shard_map.140 = (f32[2,8,4,16,128]{4,3,2,1,0:T(8,128)}, f32[8]{0:T(128)}, f32[8]{0:T(128)}) custom-call(f32[2,8,4,16,128]{4,3,2,1,0:T(8,128)S(1)} %get-tuple-element.6.applied, f32[8]{0:T(128)S(1)} %get-tuple-element.7.rayleigh, f32[8]{0:T(128)S(1)} %get-tuple-element.8.residual), custom_call_target="tpu_custom_call" | custom-call | tf_op jit(solution)/shard_map/pallas_call | solution.py:396

commit v4 on v3

--- a/solution.py
+++ b/solution.py
@@ -15,6 +15,9 @@
 NZ = 32
 ZL = N // NZ
 YL = N // NY
+ENTRY = ((0, 2), (0, 6), (2, 0), (1, 1), (1, 7), (3, 1), (3, 7), (1, 0), (3, 0), (0, 1), (0, 7))
+ROUNDS = (((0, 2), (0, 6), (2, 0)), ((0, 2), (0, 6)))
+SENT_IN = ((0, 1, 2, 3), (), ())
 SL = N // NZ
 CHUNKS = ((0, 0, 1), (0, 1, 1), (0, 2, 2), (1, 0, 4))
 LIVE = 112
@@ -97,7 +100,7 @@
     out, ray_ref, res_ref,
     u_in, v_in, cutoff, locked, rf, gf, lf, ri, gi, li, zf, zi,
     planes, pot, sent, got, back, ret, wave, app, kin, row1, row2, tot1, tot2,
-    in_sem, y_send, y_recv, z_send, z_recv, b_send, b_recv, o_send, o_recv, own, r_send, r_recv,
+    in_sem, y_send, y_recv, z_send, z_recv, b_send, b_recv, o_send, o_recv, own, r_send, r_recv, rounds,
 ):
     my = lax.axis_index("py")
     mz = lax.axis_index("pz")
@@ -107,7 +110,7 @@
     y_peers = [y_chip[d] + y_core[c] for d in (2, 1, 3, 0) for c in (0, 1) if d or c]
     z_x = [lax.rem(mz // 8 + d, 4) * 8 for d in range(4)]
     z_z = [lax.rem(mz + d, 8) for d in range(8)]
-    z_peers = [(z_x[d] + z_z[e], e % 2) for e in (4, 3, 5, 2, 6, 1, 7, 0) for d in (2, 1, 3, 0) if d or e]
+    z_peers = [(z_x[d] + z_z[e], e % 2) for d in (2, 1, 3, 0) for e in (4, 3, 5, 2, 6, 1, 7, 0) if d or e]
 
     def load(i, source, target):
         copy = pltpu.make_async_copy(source, target, in_sem.at[i])
@@ -117,9 +120,11 @@
     first = [load(0, u_hbm, u_in), load(1, v_hbm, v_in)]
     barrier = pltpu.get_barrier_semaphore()
 
-    for d, _ in z_peers:
-        pl.semaphore_signal(barrier, inc=1, device_id=(my, d), device_id_type=MESH)
-
+    def greet(sem, offsets):
+        for d, e in offsets:
+            pl.semaphore_signal(sem, inc=1, device_id=(my, z_x[d] + z_z[e]), device_id_type=MESH)
+
+    greet(barrier, ENTRY)
     for j in y_peers:
         pl.semaphore_signal(barrier, inc=1, device_id=(j, mz), device_id_type=MESH)
 
@@ -128,20 +133,32 @@
     for copy in first:
         copy.wait()
     with jax.named_scope("barrier"):
-        pl.semaphore_wait(barrier, NZ - 1 + NY - 1)
+        pl.semaphore_wait(barrier, len(ENTRY) + NY - 1)
 
     def drain(ref, sem, name="end"):
         with jax.named_scope(name):
             pltpu.make_async_copy(ref, ref, sem).wait()
 
     mine = pl.ds(pl.multiple_of(my * YL, YL), YL)
-    for c, (part, z, nz) in enumerate(CHUNKS):
+    def y_out(c):
+        part, z, nz = CHUNKS[c]
         for j in y_peers:
             pltpu.make_async_remote_copy(
                 u_in.at[part, j, pl.ds(z, nz)], planes.at[part, pl.ds(z, nz), mine, :], y_send.at[c], y_recv.at[c],
                 device_id=(j, mz), device_id_type=MESH,
             ).start()
 
+    for r, offsets in enumerate(ROUNDS):
+        if r:
+            with jax.named_scope(f"round{r}"):
+                pl.semaphore_wait(rounds.at[r - 1], len(ROUNDS[r - 1]))
+        greet(rounds.at[r], offsets)
+        for c in SENT_IN[r]:
+            y_out(c)
+    with jax.named_scope("roundlast"):
+        pl.semaphore_wait(rounds.at[len(ROUNDS) - 1], len(ROUNDS[-1]))
+    for c in SENT_IN[len(ROUNDS)]:
+        y_out(c)
     for j in y_peers:
         pltpu.make_async_remote_copy(
             v_in, pot.at[:, mine, :], y_send.at[len(CHUNKS)], y_recv.at[len(CHUNKS)],
@@ -161,6 +178,78 @@
     lane = lax.broadcasted_iota(jnp.int32, (1, N), 1)
     up = (lane + 1) // 2
     down = (N - lane) // 2
+    others = pl.ds(0, (NY - 1) * YL)
+    own_row = HOST + lax.broadcasted_iota(jnp.int32, (FOLD, N), 0) // 2
+    own_kx = (lax.broadcasted_iota(jnp.int32, (FOLD, N), 1) + 1) // 2
+    holds = own_row * own_row + own_kx * own_kx <= SPHERE
+
+    def plane_transform(field, target, part, first, count):
+        x = times_left(lf[...], jnp.concatenate([field[z] for z in range(count)], axis=1))
+        x = [x[:, z * N : (z + 1) * N] for z in range(count)]
+        guest = times_right(jnp.concatenate([a[LIVE:] for a in x], axis=0), gf[...])
+        live = times_right(jnp.concatenate([a[:LIVE] for a in x], axis=0), rf[...])
+        for z in range(count):
+            a = live[z * LIVE : (z + 1) * LIVE]
+            target[part, first + z, :FOLD, :] = jnp.where(holds, a[:FOLD], guest[z * FOLD : (z + 1) * FOLD])
+            target[part, first + z, FOLD:, :] = a[FOLD:]
+
+    def by_parity(act):
+        for odd in range(2):
+            pl.when(lax.rem(mz, 2) == odd)(functools.partial(act, odd))
+
+    got_view = got.reshape(2, NZ, ZL, SL, N)
+    back_view = back.reshape(2, NZ, ZL, SL, N)
+
+    def z_out(part, first, count, c, odd):
+        def copy_of(d, o):
+            n = slots(o, part)
+            return (
+                sent.at[part, pl.ds(first, count), pl.ds(first_slot(d, o, part), n), :],
+                got_view.at[part, mz, pl.ds(first, count), pl.ds(0, n), :],
+            )
+
+        for d, e in z_peers:
+            a, b = copy_of(d, (odd + e) % 2)
+            pltpu.make_async_remote_copy(
+                a, b, z_send.at[part], z_recv.at[part], device_id=(my, d), device_id_type=MESH
+            ).start()
+        pltpu.make_async_copy(*copy_of(mz, odd), own.at[c]).start()
+
+    def z_back(part, odd):
+        n = slots(odd, part)
+        target = ret.at[part, :, pl.ds(first_slot(mz, odd, part), n), :]
+        for d, _ in z_peers:
+            pltpu.make_async_remote_copy(
+                back_view.at[part, d, :, pl.ds(0, n), :], target, b_send.at[part], b_recv.at[part],
+                device_id=(my, d), device_id_type=MESH,
+            ).start()
+        pltpu.make_async_copy(back_view.at[part, mz, :, pl.ds(0, n), :], target, own.at[len(CHUNKS) + part]).start()
+
+    def z_rows(part, odd):
+        return got_view.at[part, pl.ds(0, NZ - 1), :, pl.ds(0, slots(odd, part)), :]
+
+    def slot_rows(part, odd):
+        return ret.at[part, :, pl.ds(0, LIVE - slots(odd, part)), :]
+
+    def own_wait(part, count, c, odd):
+        a = ret.at[part, pl.ds(0, count), pl.ds(0, slots(odd, part)), :]
+        pltpu.make_async_copy(a, a, own.at[c]).wait()
+
+    def z_wait(part, odd):
+        drain(z_rows(part, odd), z_recv.at[part], f"z{part}")
+        for c, (p, _, count) in enumerate(CHUNKS):
+            if p == part:
+                own_wait(part, count, c, odd)
+
+    def b_wait(part, odd):
+        drain(slot_rows(part, odd), b_recv.at[part], f"b{part}")
+        own_wait(part, ZL, len(CHUNKS) + part, odd)
+
+    for c, (part, z, nz) in enumerate(CHUNKS):
+        drain(planes.at[part, pl.ds(z, nz), others, :], y_recv.at[c], f"y{c}")
+        plane_transform(planes[part, z : z + nz], sent, part, z, nz)
+        by_parity(functools.partial(z_out, part, z, nz, c))
+
     for part in range(2):
         start = first_slot(mz, lax.rem(mz, 2), part)
         for i in range(SL):
@@ -174,78 +263,6 @@
             kin[part, :, i * N : (i + 1) * N] = jnp.where(
                 s <= cutoff[0], 0.5 * (math.pi / N) ** 2 * s.astype(F32), 0.0
             )
-
-    others = pl.ds(0, (NY - 1) * YL)
-    own_row = HOST + lax.broadcasted_iota(jnp.int32, (FOLD, N), 0) // 2
-    own_kx = (lax.broadcasted_iota(jnp.int32, (FOLD, N), 1) + 1) // 2
-    holds = own_row * own_row + own_kx * own_kx <= SPHERE
-
-    def plane_transform(field, target, part, first, count):
-        x = times_left(lf[...], jnp.concatenate([field[z] for z in range(count)], axis=1))
-        x = [x[:, z * N : (z + 1) * N] for z in range(count)]
-        guest = times_right(jnp.concatenate([a[LIVE:] for a in x], axis=0), gf[...])
-        live = times_right(jnp.concatenate([a[:LIVE] for a in x], axis=0), rf[...])
-        for z in range(count):
-            a = live[z * LIVE : (z + 1) * LIVE]
-            target[part, first + z, :FOLD, :] = jnp.where(holds, a[:FOLD], guest[z * FOLD : (z + 1) * FOLD])
-            target[part, first + z, FOLD:, :] = a[FOLD:]
-
-    def by_parity(act):
-        for odd in range(2):
-            pl.when(lax.rem(mz, 2) == odd)(functools.partial(act, odd))
-
-    got_view = got.reshape(2, NZ, ZL, SL, N)
-    back_view = back.reshape(2, NZ, ZL, SL, N)
-
-    def z_out(part, first, count, c, odd):
-        def copy_of(d, o):
-            n = slots(o, part)
-            return (
-                sent.at[part, pl.ds(first, count), pl.ds(first_slot(d, o, part), n), :],
-                got_view.at[part, mz, pl.ds(first, count), pl.ds(0, n), :],
-            )
-
-        for d, e in z_peers:
-            a, b = copy_of(d, (odd + e) % 2)
-            pltpu.make_async_remote_copy(
-                a, b, z_send.at[part], z_recv.at[part], device_id=(my, d), device_id_type=MESH
-            ).start()
-        pltpu.make_async_copy(*copy_of(mz, odd), own.at[c]).start()
-
-    def z_back(part, odd):
-        n = slots(odd, part)
-        target = ret.at[part, :, pl.ds(first_slot(mz, odd, part), n), :]
-        for d, _ in z_peers:
-            pltpu.make_async_remote_copy(
-                back_view.at[part, d, :, pl.ds(0, n), :], target, b_send.at[part], b_recv.at[part],
-                device_id=(my, d), device_id_type=MESH,
-            ).start()
-        pltpu.make_async_copy(back_view.at[part, mz, :, pl.ds(0, n), :], target, own.at[len(CHUNKS) + part]).start()
-
-    def z_rows(part, odd):
-        return got_view.at[part, pl.ds(0, NZ - 1), :, pl.ds(0, slots(odd, part)), :]
-
-    def slot_rows(part, odd):
-        return ret.at[part, :, pl.ds(0, LIVE - slots(odd, part)), :]
-
-    def own_wait(part, count, c, odd):
-        a = ret.at[part, pl.ds(0, count), pl.ds(0, slots(odd, part)), :]
-        pltpu.make_async_copy(a, a, own.at[c]).wait()
-
-    def z_wait(part, odd):
-        drain(z_rows(part, odd), z_recv.at[part], f"z{part}")
-        for c, (p, _, count) in enumerate(CHUNKS):
-            if p == part:
-                own_wait(part, count, c, odd)
-
-    def b_wait(part, odd):
-        drain(slot_rows(part, odd), b_recv.at[part], f"b{part}")
-        own_wait(part, ZL, len(CHUNKS) + part, odd)
-
-    for c, (part, z, nz) in enumerate(CHUNKS):
-        drain(planes.at[part, pl.ds(z, nz), others, :], y_recv.at[c], f"y{c}")
-        plane_transform(planes[part, z : z + nz], sent, part, z, nz)
-        by_parity(functools.partial(z_out, part, z, nz, c))
 
     def folded(x):
         return jnp.sum(x.reshape(-1, 8, N), axis=0)
@@ -390,6 +407,7 @@
             dma((12,)),
             dma((len(CHUNKS) + 1,)), dma((len(CHUNKS) + 1,)), dma((2,)), dma((2,)), dma((2,)), dma((2,)),
             dma((2,)), dma((2,)), dma((len(CHUNKS) + 2,)), dma((2,)), dma((2,)),
+            pltpu.SemaphoreType.REGULAR((len(ROUNDS),)),
         ],
         compiler_params=pltpu.CompilerParams(collective_id=0, has_side_effects=True),
     )(wavefunctions, potential, cutoff_sq, locked_mask, *consts)

time: 51.4 us -> 49.3 us (0.959)
  Pallas kernels: 50 us -> 47.9 us
    pallas_call x1, Pallas kernels: 49.2 us -> 47.1 us  [body(): pl.pallas_call(kernel, out_shape=(pltpu.VMEM((2, NB, ZL, YL, N), F32), pl...]
where the time goes in v4:
time: 49.3 us; the launch traced here: 49.2 us
  Pallas kernels  47.9 us (97%)
  between operations  1.28 us (3%)
    pallas_call x1, Pallas kernels, body(): pl.pallas_call(kernel, out_shape=(pltpu.VMEM((2, NB, ZL, YL, N), F32), pl...  47.1 us

profile of v4, /device:TPU:1, one launch (start us, length us, event | category | flops | bytes accessed | tf_op | source)
XLA Modules:
  0.0 49.2 jit_solution(15378763547185931752)
XLA Ops:
  1.3 47.1 %shard_map.139 = (f32[2,8,4,16,128]{4,3,2,1,0:T(8,128)S(1)}, f32[8]{0:T(128)S(1)}, f32[8]{0:T(128)S(1)}) custom-call(f32[2,8,4,16,128]{4,3,2,1,0:T(8,128)} %u_hbm.1, f32[4,16,128]{2,1,0:T(8,128)} %v_hbm.1, s32[1]{0:T(128)S(6)} %copy.15.cutoff_hbm, s32[8]{0:T(128)} %locked_hbm.1, bf16[256,256]{1,0:T(8,128)(2,1)} %constant.16.clone.rf_hbm, ...), custom_call_target="tpu_custom_call" | custom-call | tf_op jit(solution)/shard_map/pallas_call | solution.py:379
  48.4 0.8 %shard_map.140 = (f32[2,8,4,16,128]{4,3,2,1,0:T(8,128)}, f32[8]{0:T(128)}, f32[8]{0:T(128)}) custom-call(f32[2,8,4,16,128]{4,3,2,1,0:T(8,128)S(1)} %get-tuple-element.6.applied, f32[8]{0:T(128)S(1)} %get-tuple-element.7.rayleigh, f32[8]{0:T(128)S(1)} %get-tuple-element.8.residual), custom_call_target="tpu_custom_call" | custom-call | tf_op jit(solution)/shard_map/pallas_call | solution.py:414

commit v5 on v4

--- a/solution.py
+++ b/solution.py
@@ -1,4 +1,5 @@
 import functools
+import itertools
 import math
 
 import jax
@@ -18,6 +19,8 @@
 ENTRY = ((0, 2), (0, 6), (2, 0), (1, 1), (1, 7), (3, 1), (3, 7), (1, 0), (3, 0), (0, 1), (0, 7))
 ROUNDS = (((0, 2), (0, 6), (2, 0)), ((0, 2), (0, 6)))
 SENT_IN = ((0, 1, 2, 3), (), ())
+BACKS = ((0, 0, 4), (1, 0, 4))
+TOLD = 64
 SL = N // NZ
 CHUNKS = ((0, 0, 1), (0, 1, 1), (0, 2, 2), (1, 0, 4))
 LIVE = 112
@@ -99,8 +102,8 @@
     u_hbm, v_hbm, cutoff_hbm, locked_hbm, rf_hbm, gf_hbm, lf_hbm, ri_hbm, gi_hbm, li_hbm, zf_hbm, zi_hbm,
     out, ray_ref, res_ref,
     u_in, v_in, cutoff, locked, rf, gf, lf, ri, gi, li, zf, zi,
-    planes, pot, sent, got, back, ret, wave, app, kin, row1, row2, tot1, tot2,
-    in_sem, y_send, y_recv, z_send, z_recv, b_send, b_recv, o_send, o_recv, own, r_send, r_recv, rounds,
+    planes, pot, sent, got, back, ret, wave, app, kin, row1, sums,
+    in_sem, y_send, y_recv, z_send, z_recv, b_send, b_recv, o_send, o_recv, own, r_send, r_recv, r_own, rounds,
 ):
     my = lax.axis_index("py")
     mz = lax.axis_index("pz")
@@ -176,6 +179,7 @@
         return 4 - (odd + part) % 2
 
     lane = lax.broadcasted_iota(jnp.int32, (1, N), 1)
+    mine_row = pl.ds(mz * NY + my, 1)
     up = (lane + 1) // 2
     down = (N - lane) // 2
     others = pl.ds(0, (NY - 1) * YL)
@@ -215,21 +219,24 @@
             ).start()
         pltpu.make_async_copy(*copy_of(mz, odd), own.at[c]).start()
 
-    def z_back(part, odd):
+    def z_back(c, odd):
+        part, first, count = BACKS[c]
         n = slots(odd, part)
-        target = ret.at[part, :, pl.ds(first_slot(mz, odd, part), n), :]
+        target = ret.at[part, pl.ds(first, count), pl.ds(first_slot(mz, odd, part), n), :]
         for d, _ in z_peers:
             pltpu.make_async_remote_copy(
-                back_view.at[part, d, :, pl.ds(0, n), :], target, b_send.at[part], b_recv.at[part],
+                back_view.at[part, d, pl.ds(first, count), pl.ds(0, n), :], target, b_send.at[c], b_recv.at[c],
                 device_id=(my, d), device_id_type=MESH,
             ).start()
-        pltpu.make_async_copy(back_view.at[part, mz, :, pl.ds(0, n), :], target, own.at[len(CHUNKS) + part]).start()
-
-    def z_rows(part, odd):
-        return got_view.at[part, pl.ds(0, NZ - 1), :, pl.ds(0, slots(odd, part)), :]
-
-    def slot_rows(part, odd):
-        return ret.at[part, :, pl.ds(0, LIVE - slots(odd, part)), :]
+        pltpu.make_async_copy(
+            back_view.at[part, mz, pl.ds(first, count), pl.ds(0, n), :], target, own.at[len(CHUNKS) + c]
+        ).start()
+
+    def z_rows(part, odd, count=ZL):
+        return got_view.at[part, pl.ds(0, NZ - 1), pl.ds(0, count), pl.ds(0, slots(odd, part)), :]
+
+    def slot_rows(part, odd, count=ZL):
+        return ret.at[part, pl.ds(0, count), pl.ds(0, LIVE - slots(odd, part)), :]
 
     def own_wait(part, count, c, odd):
         a = ret.at[part, pl.ds(0, count), pl.ds(0, slots(odd, part)), :]
@@ -241,9 +248,10 @@
             if p == part:
                 own_wait(part, count, c, odd)
 
-    def b_wait(part, odd):
-        drain(slot_rows(part, odd), b_recv.at[part], f"b{part}")
-        own_wait(part, ZL, len(CHUNKS) + part, odd)
+    def b_wait(c, odd):
+        part, _, count = BACKS[c]
+        drain(slot_rows(part, odd, count), b_recv.at[c], f"b{c}")
+        own_wait(part, count, len(CHUNKS) + c, odd)
 
     for c, (part, z, nz) in enumerate(CHUNKS):
         drain(planes.at[part, pl.ds(z, nz), others, :], y_recv.at[c], f"y{c}")
@@ -288,78 +296,82 @@
         for z in range(ZL):
             for i in range(SL):
                 back[part, pl.ds(SL * z + i, NZ, stride=SL * ZL), :] = x[z * NZ : (z + 1) * NZ, i * N : (i + 1) * N]
-        by_parity(functools.partial(z_back, part))
-
-    for part in range(2):
-        by_parity(functools.partial(b_wait, part))
-        x = ret[part]
-        corr = corr + folded(sent[part] * x)
-        square = square + folded(x * (x + 2.0 * wave[part]))
-        if part == 1:
+        for c, back_chunk in enumerate(BACKS):
+            if back_chunk[0] == part:
+                by_parity(functools.partial(z_back, c))
+
+    def tell(offsets):
+        for a, b, d, e in offsets:
+            pltpu.make_async_remote_copy(
+                row1, sums.at[mine_row, :], r_send.at[0], r_recv.at[0],
+                device_id=(y_chip[a] + y_core[b], z_x[d] + z_z[e]), device_id_type=MESH,
+            ).start()
+
+    everyone = sorted(
+        [p for p in itertools.product(range(4), range(2), range(4), range(8)) if any(p)],
+        key=lambda p: -4 * (min(p[0], 4 - p[0]) + min(p[2], 4 - p[2]) + min(p[3], 8 - p[3])) - p[1],
+    )
+    for c, (part, first, count) in enumerate(BACKS):
+        by_parity(functools.partial(b_wait, c))
+        some = pl.ds(first, count)
+        x = ret[part, some]
+        corr = corr + folded(sent[part, some] * x)
+        square = square + folded(x * (x + 2.0 * wave[part, some]))
+        last = c == len(BACKS) - 1
+        if last:
             row = jnp.zeros((1, N), F32)
             for i, value in enumerate((norm, corr, square)):
                 total = jnp.sum(jnp.sum(value, axis=0, keepdims=True), axis=1, keepdims=True)
-                row = jnp.where(lane == 16 * i + my, total, row)
+                row = jnp.where(lane == i, total, row)
             row1[...] = row
-            tot1[mz] = row
-
-            for d, _ in z_peers:
-                pltpu.make_async_remote_copy(
-                    row1, tot1.at[mz], r_send.at[0], r_recv.at[0], device_id=(my, d), device_id_type=MESH
-                ).start()
-
-        x = [ret[part, z] for z in range(ZL)]
+            tell(everyone[:TOLD])
+        x = [ret[part, first + z] for z in range(count)]
         guest = times_right(jnp.concatenate([jnp.where(holds, 0.0, a[:FOLD]) for a in x], axis=0), gi[...])
         live = [b for a in x for b in (jnp.where(holds, a[:FOLD], 0.0), a[FOLD:])]
         live = times_right(jnp.concatenate(live, axis=0), ri[...])
         x = [
             jnp.concatenate([live[z * LIVE : (z + 1) * LIVE], guest[z * FOLD : (z + 1) * FOLD]], axis=0)
-            for z in range(ZL)
+            for z in range(count)
         ]
         x = times_left(li[...], jnp.concatenate(x, axis=1))
-        for z in range(ZL):
-            app[part, z] = x[:, z * N : (z + 1) * N] + pot[z] * planes[part, z]
-
+        for z in range(count):
+            app[part, first + z] = x[:, z * N : (z + 1) * N] + pot[first + z] * planes[part, first + z]
         for j in y_peers:
             pltpu.make_async_remote_copy(
-                app.at[part, :, pl.ds(pl.multiple_of(j * YL, YL), YL), :], out.at[part, my],
-                o_send.at[part], o_recv.at[part],
+                app.at[part, some, pl.ds(pl.multiple_of(j * YL, YL), YL), :], out.at[part, my, some],
+                o_send.at[c], o_recv.at[c],
                 device_id=(j, mz), device_id_type=MESH,
             ).start()
-        out[part, my] = app[part, :, mine, :]
-
-    drain(tot1.at[pl.ds(0, NZ - 1)], r_recv.at[0], "r0")
-    row = jnp.sum(tot1[...], axis=0)
-    row2[...] = row
-    tot2[my] = row
-
-    for j in y_peers:
-        pltpu.make_async_remote_copy(
-            row2, tot2.at[my], r_send.at[1], r_recv.at[1], device_id=(j, mz), device_id_type=MESH
-        ).start()
+        if last:
+            tell(everyone[TOLD:])
+            pltpu.make_async_copy(row1, sums.at[mine_row, :], r_own).start()
+        out[part, my, some] = app[part, some, mine, :]
 
     for part in range(2):
         by_parity(lambda odd, part=part: drain(slot_rows(part, odd), z_send.at[part]))
-        by_parity(lambda odd, part=part: drain(z_rows(part, odd), b_send.at[part]))
-        drain(app.at[part, :, others, :], o_send.at[part])
-        drain(out.at[part, pl.ds(0, NY - 1)], o_recv.at[part], f"o{part}")
+    for c, (part, first, count) in enumerate(BACKS):
+        by_parity(lambda odd, c=c, part=part, count=count: drain(z_rows(part, odd, count), b_send.at[c]))
+        drain(app.at[part, pl.ds(first, count), others, :], o_send.at[c], f"s{c}")
+        drain(out.at[part, pl.ds(0, NY - 1), pl.ds(first, count)], o_recv.at[c], f"o{c}")
     drain(pot.at[:, others, :], y_send.at[len(CHUNKS)])
     for c, (part, z, nz) in enumerate(CHUNKS):
         drain(planes.at[part, pl.ds(z, nz), others, :], y_send.at[c])
-    drain(tot1.at[pl.ds(0, NZ - 1)], r_send.at[0])
-
-    keep = jnp.zeros((1, NB), F32)
+
+    told = sums.at[pl.ds(0, NY * NZ - 1), :]
+    drain(told, r_send.at[0])
+    pltpu.make_async_copy(row1, sums.at[mine_row, :], r_own).wait()
+    band = lax.broadcasted_iota(jnp.int32, (NB, NB), 0)
+    same = band == lax.broadcasted_iota(jnp.int32, (NB, NB), 1)
+    keep = jnp.zeros((NB, NB), F32)
     for b in range(NB):
-        keep = jnp.where(lane[:, :NB] == b, 1.0 - locked[b].astype(F32), keep)
-    drain(tot2.at[pl.ds(0, NY - 1)], r_recv.at[1], "r1")
-    row = jnp.sum(tot2[...], axis=0)
-    norm = row[:, 0:NB]
-    corr = row[:, 16 : 16 + NB]
-    square = row[:, 32 : 32 + NB]
+        keep = jnp.where(band == b, 1.0 - locked[b].astype(F32), keep)
+    drain(told, r_recv.at[0], "r0")
+    total = jnp.sum(sums[...].reshape(NZ, NY, N), axis=0)
+    norm, corr, square = (jnp.broadcast_to(total[:, i : i + 1], (NB, NB)) for i in range(3))
     rayleigh = corr / norm
-    ray_ref[...] = rayleigh.reshape(NB)
-    res_ref[...] = (jnp.sqrt((square - rayleigh * corr) / norm) * keep).reshape(NB)
-    drain(tot2.at[pl.ds(0, NY - 1)], r_send.at[1])
+    residual = jnp.sqrt((square - rayleigh * corr) / norm) * keep
+    ray_ref[...] = jnp.sum(jnp.where(same, rayleigh, 0.0), axis=0)
+    res_ref[...] = jnp.sum(jnp.where(same, residual, 0.0), axis=0)
 
 
 def write_out(applied, rayleigh, residual, *rest):
@@ -401,12 +413,10 @@
             pltpu.VMEM((2, ZL, N, N), F32),
             pltpu.VMEM((2, N, SL * N), F32),
             pltpu.VMEM((1, N), F32),
-            pltpu.VMEM((1, N), F32),
-            pltpu.VMEM((NZ, 1, N), F32),
-            pltpu.VMEM((NY, 1, N), F32),
+            pltpu.VMEM((NZ * NY, N), F32),
             dma((12,)),
-            dma((len(CHUNKS) + 1,)), dma((len(CHUNKS) + 1,)), dma((2,)), dma((2,)), dma((2,)), dma((2,)),
-            dma((2,)), dma((2,)), dma((len(CHUNKS) + 2,)), dma((2,)), dma((2,)),
+            dma((len(CHUNKS) + 1,)), dma((len(CHUNKS) + 1,)), dma((2,)), dma((2,)), dma((len(BACKS),)), dma((len(BACKS),)),
+            dma((len(BACKS),)), dma((len(BACKS),)), dma((len(CHUNKS) + len(BACKS),)), dma((1,)), dma((1,)), dma(()),
             pltpu.SemaphoreType.REGULAR((len(ROUNDS),)),
         ],
         compiler_params=pltpu.CompilerParams(collective_id=0, has_side_effects=True),

time: 49.3 us -> 47.5 us (0.963)
  Pallas kernels: 47.9 us -> 46.1 us
    pallas_call x1, Pallas kernels: 47.1 us -> 45.3 us  [body(): pl.pallas_call(kernel, out_shape=(pltpu.VMEM((2, NB, ZL, YL, N), F32), pl...]
where the time goes in v5:
time: 47.5 us; the launch traced here: 47.4 us
  Pallas kernels  46.1 us (97%)
  between operations  1.28 us (3%)
    pallas_call x1, Pallas kernels, body(): pl.pallas_call(kernel, out_shape=(pltpu.VMEM((2, NB, ZL, YL, N), F32), pl...  45.3 us

profile of v5, /device:TPU:1, one launch (start us, length us, event | category | flops | bytes accessed | tf_op | source)
XLA Modules:
  0.0 47.4 jit_solution(8403505399276622473)
XLA Ops:
  1.3 45.3 %shard_map.139 = (f32[2,8,4,16,128]{4,3,2,1,0:T(8,128)S(1)}, f32[8]{0:T(128)S(1)}, f32[8]{0:T(128)S(1)}) custom-call(f32[2,8,4,16,128]{4,3,2,1,0:T(8,128)} %u_hbm.1, f32[4,16,128]{2,1,0:T(8,128)} %v_hbm.1, s32[1]{0:T(128)S(6)} %copy.15.cutoff_hbm, s32[8]{0:T(128)} %locked_hbm.1, bf16[256,256]{1,0:T(8,128)(2,1)} %constant.16.clone.rf_hbm, ...), custom_call_target="tpu_custom_call" | custom-call | tf_op jit(solution)/shard_map/pallas_call | solution.py:391
  46.5 0.8 %shard_map.140 = (f32[2,8,4,16,128]{4,3,2,1,0:T(8,128)}, f32[8]{0:T(128)}, f32[8]{0:T(128)}) custom-call(f32[2,8,4,16,128]{4,3,2,1,0:T(8,128)S(1)} %get-tuple-element.6.applied, f32[8]{0:T(128)S(1)} %get-tuple-element.7.rayleigh, f32[8]{0:T(128)S(1)} %get-tuple-element.8.residual), custom_call_target="tpu_custom_call" | custom-call | tf_op jit(solution)/shard_map/pallas_call | solution.py:424

commit v6 on v5

--- a/solution.py
+++ b/solution.py
@@ -100,9 +100,9 @@
 
 def kernel(
     u_hbm, v_hbm, cutoff_hbm, locked_hbm, rf_hbm, gf_hbm, lf_hbm, ri_hbm, gi_hbm, li_hbm, zf_hbm, zi_hbm,
-    out, ray_ref, res_ref,
+    out, sums, keep_ref,
     u_in, v_in, cutoff, locked, rf, gf, lf, ri, gi, li, zf, zi,
-    planes, pot, sent, got, back, ret, wave, app, kin, row1, sums,
+    planes, pot, sent, got, back, ret, wave, app, kin, row1,
     in_sem, y_send, y_recv, z_send, z_recv, b_send, b_recv, o_send, o_recv, own, r_send, r_recv, r_own, rounds,
 ):
     my = lax.axis_index("py")
@@ -113,7 +113,11 @@
     y_peers = [y_chip[d] + y_core[c] for d in (2, 1, 3, 0) for c in (0, 1) if d or c]
     z_x = [lax.rem(mz // 8 + d, 4) * 8 for d in range(4)]
     z_z = [lax.rem(mz + d, 8) for d in range(8)]
-    z_peers = [(z_x[d] + z_z[e], e % 2) for d in (2, 1, 3, 0) for e in (4, 3, 5, 2, 6, 1, 7, 0) if d or e]
+    by_hops = sorted(
+        [p for p in itertools.product((2, 1, 3, 0), (4, 3, 5, 2, 6, 1, 7, 0)) if any(p)],
+        key=lambda p: -min(p[0], 4 - p[0]) - min(p[1], 8 - p[1]),
+    )
+    z_peers = [(z_x[d] + z_z[e], e % 2) for d, e in by_hops]
 
     def load(i, source, target):
         copy = pltpu.make_async_copy(source, target, in_sem.at[i])
@@ -361,25 +365,27 @@
     drain(told, r_send.at[0])
     pltpu.make_async_copy(row1, sums.at[mine_row, :], r_own).wait()
     band = lax.broadcasted_iota(jnp.int32, (NB, NB), 0)
-    same = band == lax.broadcasted_iota(jnp.int32, (NB, NB), 1)
     keep = jnp.zeros((NB, NB), F32)
     for b in range(NB):
         keep = jnp.where(band == b, 1.0 - locked[b].astype(F32), keep)
+    keep_ref[...] = keep
     drain(told, r_recv.at[0], "r0")
+
+
+def write_out(applied, sums, keep, out, ray_hbm, res_hbm, ray, res, sem):
+    first = pltpu.make_async_copy(applied, out, sem.at[0])
+    first.start()
+    same = lax.broadcasted_iota(jnp.int32, (NB, NB), 0) == lax.broadcasted_iota(jnp.int32, (NB, NB), 1)
     total = jnp.sum(sums[...].reshape(NZ, NY, N), axis=0)
     norm, corr, square = (jnp.broadcast_to(total[:, i : i + 1], (NB, NB)) for i in range(3))
     rayleigh = corr / norm
-    residual = jnp.sqrt((square - rayleigh * corr) / norm) * keep
-    ray_ref[...] = jnp.sum(jnp.where(same, rayleigh, 0.0), axis=0)
-    res_ref[...] = jnp.sum(jnp.where(same, residual, 0.0), axis=0)
-
-
-def write_out(applied, rayleigh, residual, *rest):
-    sources, sem = (applied, rayleigh, residual), rest[3]
-    copies = [pltpu.make_async_copy(a, b, sem.at[i]) for i, (a, b) in enumerate(zip(sources, rest[:3], strict=True))]
+    residual = jnp.sqrt((square - rayleigh * corr) / norm) * keep[...]
+    ray[...] = jnp.sum(jnp.where(same, rayleigh, 0.0), axis=0)
+    res[...] = jnp.sum(jnp.where(same, residual, 0.0), axis=0)
+    copies = [pltpu.make_async_copy(ray, ray_hbm, sem.at[1]), pltpu.make_async_copy(res, res_hbm, sem.at[2])]
     for copy in copies:
         copy.start()
-    for copy in copies:
+    for copy in [first, *copies]:
         copy.wait()
 
 
@@ -388,12 +394,12 @@
     hbm = pl.BlockSpec(memory_space=pltpu.HBM)
     vmem = pl.BlockSpec(memory_space=pltpu.VMEM)
     dma = pltpu.SemaphoreType.DMA
-    applied, rayleigh, residual = pl.pallas_call(
+    results = pl.pallas_call(
         kernel,
         out_shape=(
             pltpu.VMEM((2, NB, ZL, YL, N), F32),
-            pltpu.VMEM((NB,), F32),
-            pltpu.VMEM((NB,), F32),
+            pltpu.VMEM((NZ * NY, N), F32),
+            pltpu.VMEM((NB, NB), F32),
         ),
         in_specs=[hbm] * 12,
         out_specs=(vmem, vmem, vmem),
@@ -413,7 +419,6 @@
             pltpu.VMEM((2, ZL, N, N), F32),
             pltpu.VMEM((2, N, SL * N), F32),
             pltpu.VMEM((1, N), F32),
-            pltpu.VMEM((NZ * NY, N), F32),
             dma((12,)),
             dma((len(CHUNKS) + 1,)), dma((len(CHUNKS) + 1,)), dma((2,)), dma((2,)), dma((len(BACKS),)), dma((len(BACKS),)),
             dma((len(BACKS),)), dma((len(BACKS),)), dma((len(CHUNKS) + len(BACKS),)), dma((1,)), dma((1,)), dma(()),
@@ -430,8 +435,8 @@
         ),
         in_specs=[vmem] * 3,
         out_specs=(hbm,) * 3,
-        scratch_shapes=[dma((3,))],
-    )(*[pltpu.with_memory_space_constraint(a, pltpu.VMEM) for a in (applied, rayleigh, residual)])
+        scratch_shapes=[pltpu.VMEM((NB,), F32), pltpu.VMEM((NB,), F32), dma((3,))],
+    )(*[pltpu.with_memory_space_constraint(a, pltpu.VMEM) for a in results])
 
 
 def solution(mesh):

time: 47.5 us -> 47.2 us (level)
  no operation moved by 1% of the time
where the time goes in v6:
time: 47.2 us; the launch traced here: 47.1 us
  Pallas kernels  45.8 us (97%)
  between operations  1.28 us (3%)
    pallas_call x1, Pallas kernels, body(): pl.pallas_call(kernel, out_shape=(pltpu.VMEM((2, NB, ZL, YL, N), F32), pl...  45 us

profile of v6, /device:TPU:1, one launch (start us, length us, event | category | flops | bytes accessed | tf_op | source)
XLA Modules:
  0.0 47.1 jit_solution(11129966622963598477)
XLA Ops:
  1.3 45.0 %shard_map.139 = (f32[2,8,4,16,128]{4,3,2,1,0:T(8,128)S(1)}, f32[256,128]{1,0:T(8,128)S(1)}, f32[8,8]{1,0:T(8,128)S(1)}) custom-call(f32[2,8,4,16,128]{4,3,2,1,0:T(8,128)} %u_hbm.1, f32[4,16,128]{2,1,0:T(8,128)} %v_hbm.1, s32[1]{0:T(128)S(6)} %copy.15.cutoff_hbm, s32[8]{0:T(128)} %locked_hbm.1, bf16[256,256]{1,0:T(8,128)(2,1)} %constant.16.clone.rf_hbm, ...), custom_call_target="tpu_custom_call" | custom-call | tf_op jit(solution)/shard_map/pallas_call | solution.py:397
  46.3 0.8 %shard_map.140 = (f32[2,8,4,16,128]{4,3,2,1,0:T(8,128)}, f32[8]{0:T(128)}, f32[8]{0:T(128)}) custom-call(f32[2,8,4,16,128]{4,3,2,1,0:T(8,128)S(1)} %get-tuple-element.6.applied, f32[256,128]{1,0:T(8,128)S(1)} %get-tuple-element.7.sums, f32[8,8]{1,0:T(8,128)S(1)} %get-tuple-element.8.keep), custom_call_target="tpu_custom_call" | custom-call | tf_op jit(solution)/shard_map/pallas_call | solution.py:429

commit v7 on v6

--- a/solution.py
+++ b/solution.py
@@ -162,15 +162,16 @@
         greet(rounds.at[r], offsets)
         for c in SENT_IN[r]:
             y_out(c)
+        if r == 0:
+            for j in y_peers:
+                pltpu.make_async_remote_copy(
+                    v_in, pot.at[:, mine, :], y_send.at[len(CHUNKS)], y_recv.at[len(CHUNKS)],
+                    device_id=(j, mz), device_id_type=MESH,
+                ).start()
     with jax.named_scope("roundlast"):
         pl.semaphore_wait(rounds.at[len(ROUNDS) - 1], len(ROUNDS[-1]))
     for c in SENT_IN[len(ROUNDS)]:
         y_out(c)
-    for j in y_peers:
-        pltpu.make_async_remote_copy(
-            v_in, pot.at[:, mine, :], y_send.at[len(CHUNKS)], y_recv.at[len(CHUNKS)],
-            device_id=(j, mz), device_id_type=MESH,
-        ).start()
     planes[:, :, mine, :] = u_in[:, my]
     pot[:, mine, :] = v_in[...]
     for copy in later:
@@ -304,6 +305,12 @@
             if back_chunk[0] == part:
                 by_parity(functools.partial(z_back, c))
 
+    def with_total(row, i, value):
+        total = jnp.sum(jnp.sum(value, axis=0, keepdims=True), axis=1, keepdims=True)
+        return jnp.where(lane == i, total, row)
+
+    row1[...] = with_total(jnp.zeros((1, N), F32), 0, norm)
+
     def tell(offsets):
         for a, b, d, e in offsets:
             pltpu.make_async_remote_copy(
@@ -323,11 +330,7 @@
         square = square + folded(x * (x + 2.0 * wave[part, some]))
         last = c == len(BACKS) - 1
         if last:
-            row = jnp.zeros((1, N), F32)
-            for i, value in enumerate((norm, corr, square)):
-                total = jnp.sum(jnp.sum(value, axis=0, keepdims=True), axis=1, keepdims=True)
-                row = jnp.where(lane == i, total, row)
-            row1[...] = row
+            row1[...] = with_total(with_total(row1[...], 1, corr), 2, square)
             tell(everyone[:TOLD])
         x = [ret[part, first + z] for z in range(count)]
         guest = times_right(jnp.concatenate([jnp.where(holds, 0.0, a[:FOLD]) for a in x], axis=0), gi[...])

time: 47.2 us -> 47.3 us (level)
  no operation moved by 1% of the time
where the time goes in v7:
time: 47.3 us; the launch traced here: 47.2 us
  Pallas kernels  45.9 us (97%)
  between operations  1.28 us (3%)
    pallas_call x1, Pallas kernels, body(): pl.pallas_call(kernel, out_shape=(pltpu.VMEM((2, NB, ZL, YL, N), F32), pl...  45.1 us

profile of v7, /device:TPU:1, one launch (start us, length us, event | category | flops | bytes accessed | tf_op | source)
XLA Modules:
  0.0 47.2 jit_solution(4055270062247788635)
XLA Ops:
  1.3 45.1 %shard_map.139 = (f32[2,8,4,16,128]{4,3,2,1,0:T(8,128)S(1)}, f32[256,128]{1,0:T(8,128)S(1)}, f32[8,8]{1,0:T(8,128)S(1)}) custom-call(f32[2,8,4,16,128]{4,3,2,1,0:T(8,128)} %u_hbm.1, f32[4,16,128]{2,1,0:T(8,128)} %v_hbm.1, s32[1]{0:T(128)S(6)} %copy.15.cutoff_hbm, s32[8]{0:T(128)} %locked_hbm.1, bf16[256,256]{1,0:T(8,128)(2,1)} %constant.16.clone.rf_hbm, ...), custom_call_target="tpu_custom_call" | custom-call | tf_op jit(solution)/shard_map/pallas_call | solution.py:400
  46.4 0.8 %shard_map.140 = (f32[2,8,4,16,128]{4,3,2,1,0:T(8,128)}, f32[8]{0:T(128)}, f32[8]{0:T(128)}) custom-call(f32[2,8,4,16,128]{4,3,2,1,0:T(8,128)S(1)} %get-tuple-element.6.applied, f32[256,128]{1,0:T(8,128)S(1)} %get-tuple-element.7.sums, f32[8,8]{1,0:T(8,128)S(1)} %get-tuple-element.8.keep), custom_call_target="tpu_custom_call" | custom-call | tf_op jit(solution)/shard_map/pallas_call | solution.py:432
